TPU v7x, 32 devices: a whole 2x2x4 slice. The times are simulated.
32 devices in a mesh: ctx: 4 (over z), shard: 4 (over y, x), dp: 2 (over core).
Axes of the slice: x: 2, y: 2, z: 4, core: 2. Of those that a mesh axis runs over, the one named last changes fastest.
Arguments:
- tokens: bfloat16 [6, 1024, 2048], P('dp', 'ctx'), may hold values from -6 to 6
- gain_attn: float32 [2048], replicated, may hold values from 0.5 to 1.5
- gain_mlp: float32 [2048], replicated, may hold values from 0.5 to 1.5
- gain_query: float32 [128], replicated, may hold values from 0.5 to 1.5
- key_norm_gain: float32 [128], replicated, may hold values from 0.5 to 1.5
- w_query: bfloat16 [2048, 4096], P(('ctx', 'dp'), 'shard'), may hold values from -0.125 to 0.125
- key_matrix: bfloat16 [2048, 512], P(('ctx', 'dp'), 'shard'), may hold values from -0.125 to 0.125
- value_matrix: bfloat16 [2048, 512], P(('ctx', 'dp'), 'shard'), may hold values from -0.125 to 0.125
- w_out: bfloat16 [2048, 4096], P(('ctx', 'dp'), 'shard'), may hold values from -1.5 to 1.5
- w_gate: bfloat16 [4, 2048, 768], P('shard', ('ctx', 'dp')), may hold values from -0.125 to 0.125
- w_up: bfloat16 [4, 2048, 768], P('shard', ('ctx', 'dp')), may hold values from -0.125 to 0.125
- w_down: bfloat16 [4, 2048, 768], P('shard', ('ctx', 'dp')), may hold values from -0.21875 to 0.21875
- expert_ids: int32 [6, 1024, 2], P('dp', ('ctx', 'shard')), may hold values from 0 to 3, all different within a row; in each aligned block of 64 rows (0 to 63, 64 to 127, ..., all dimensions but the last counted through in order) at most 48 rows name the same one
- route_weight: float32 [6, 1024, 2], P('dp', ('ctx', 'shard')), may hold values from 0.2 to 1
- cotangent: bfloat16 [6, 1024, 2048], P('dp', ('ctx', 'shard')), may hold values from -6 to 6
Outputs:
- block_out: bfloat16 [6, 1024, 2048], P('dp', ('ctx', 'shard'))
- grad_tokens: float32 [6, 1024, 2048], P('dp', ('ctx', 'shard'))
- softmax_lse: float32 [6, 32, 1024], P('dp', 'shard', 'ctx')
- route_grad: float32 [6, 1024, 2], P('dp', ('ctx', 'shard'))
- grad_gain_attn: float32 [2048], replicated
- grad_gain_mlp: float32 [2048], replicated
- grad_gain_query: float32 [128], replicated
- grad_gain_key: float32 [128], replicated
- grad_w_query: float32 [2048, 4096], P(('ctx', 'dp'), 'shard')
- grad_w_key: float32 [2048, 512], P(('ctx', 'dp'), 'shard')
- grad_w_value: float32 [2048, 512], P(('ctx', 'dp'), 'shard')
- grad_w_out: float32 [2048, 4096], P(('ctx', 'dp'), 'shard')
- grad_w_gate: float32 [4, 2048, 768], P('shard', ('ctx', 'dp'))
- grad_w_up: float32 [4, 2048, 768], P('shard', ('ctx', 'dp'))
- grad_w_down: float32 [4, 2048, 768], P('shard', ('ctx', 'dp'))
Inputs may be any that keep to these rules, and one draw needn't show every extreme that they name: `expert_ids`: each row names 2 different experts. In each aligned block of 64 rows (all leading dimensions taken in order) no expert is named by more than 48 rows, and in some block one expert is named by exactly 48 rows.
All inputs are finite; a program needn't handle non-finite values.
Results may differ from a plain program's by a relative error of at most 0.02.
Values may be sent and summed in bfloat16 or wider, within the bound.
A program may use at most 192 MiB of HBM per device.

v0:
```python
import functools

import jax
import jax.numpy as jnp
from jax import lax
from jax.experimental import pallas as pl
from jax.experimental.pallas import tpu as pltpu
from jax.sharding import PartitionSpec as P


epsilon = 1e-06
theta_base = 1000000.0
BF = jnp.bfloat16
F32 = jnp.float32


def pairs(count, k):
    return [(i, i ^ k) for i in range(count)]


def swap(value, axis, k):
    return lax.ppermute(value, axis, pairs(lax.axis_size(axis), k))


def order_of(count):
    return sorted(range(1, count), key=lambda k: -bin(k).count("1"))


def collect(value, axis):
    count = lax.axis_size(axis)
    got = {0: value}
    for k in order_of(count):
        got[k] = swap(value, axis, k)
    return [got[k] for k in range(count)]


def folded_positions(rows, count_ctx, half_block):
    block = rows // half_block
    offset = rows % half_block
    device = block // 2
    placed = jnp.where(block % 2 == 0, device, 2 * count_ctx - 1 - device)
    return placed * half_block + offset


def rope_tables(positions, head_dim):
    freq = jnp.arange(head_dim // 2, dtype=F32) * (2.0 / head_dim)
    inverse = jnp.power(jnp.float32(theta_base), -freq)
    angles = positions.astype(F32)[..., None] * inverse
    cosine, sine = jnp.cos(angles), jnp.sin(angles)
    return jnp.concatenate([cosine, cosine], -1), jnp.concatenate([-sine, sine], -1)


def inv_rms(field):
    return lax.rsqrt(jnp.mean(field * field, -1, keepdims=True) + epsilon)


def norm_backward_step(grad_normed, normed_hat, inverse, gain):
    scaled = grad_normed * gain
    return inverse * (scaled - normed_hat * jnp.mean(scaled * normed_hat, -1, keepdims=True))


def mm(a, b):
    return lax.dot_general(a, b, (((1,), (0,)), ((), ())), preferred_element_type=F32)


def mm_nt(a, b):
    return lax.dot_general(a, b, (((1,), (1,)), ((), ())), preferred_element_type=F32)


def mm_tn(a, b):
    return lax.dot_general(a, b, (((0,), (0,)), ((), ())), preferred_element_type=F32)


def turn(u, cosine, sine):
    return u * cosine + pltpu.roll(u, u.shape[-1] // 2, 1) * sine


def turn_back(u, cosine, sine):
    return u * cosine - pltpu.roll(u, u.shape[-1] // 2, 1) * sine


def key_kernel(raw_ref, gain_ref, cos_ref, sin_ref, out_ref):
    dim = gain_ref.shape[-1]
    raw = raw_ref[:, :dim]
    unit = raw * inv_rms(raw)
    out_ref[0] = turn(unit * gain_ref[...], cos_ref[...], sin_ref[...]).astype(BF)
    out_ref[1] = raw_ref[:, dim:].astype(BF)


def key_grad_kernel(count, raw_ref, gain_ref, cos_ref, sin_ref, *refs):
    parts, (out_ref, gain_out) = refs[:count], refs[count:]
    dim = gain_ref.shape[-1]
    total = parts[0][...].astype(F32)
    for part in parts[1:]:
        total = total + part[...].astype(F32)
    raw = raw_ref[:, :dim]
    inverse = inv_rms(raw)
    unit = raw * inverse
    grad = turn_back(total[0], cos_ref[...], sin_ref[...])
    gain_out[...] = jnp.sum(grad * unit, 0, keepdims=True)
    out_ref[:, :dim] = norm_backward_step(grad, unit, inverse, gain_ref[...]).astype(BF)
    out_ref[:, dim:] = total[1].astype(BF)


def natural_rows(me_s, count_s, ref, out_ref):
    own = out_ref.shape[0] // count_s
    for j in range(count_s):
        out_ref[j * own : (j + 1) * own, :] = ref[me_s ^ j, 0]


def gather_keys(me_s, me_c, kv_ref, k_nat, v_nat):
    count_c, _, count_s, _, own, _ = kv_ref.shape
    half = count_s * own // 2
    for jc in range(count_c):
        for j in range(count_s):
            row = j * own
            at = jc * half + row if row < half else (2 * count_c - 1 - jc) * half + row - half
            k_nat[at : at + own, :] = kv_ref[me_c ^ jc, 0, me_s ^ j, 0]
            v_nat[at : at + own, :] = kv_ref[me_c ^ jc, 1, me_s ^ j, 0]


def masks(me_c, count_c, half):
    length = count_c * half
    key = lax.broadcasted_iota(jnp.int32, (length, half), 0)
    lane = lax.broadcasted_iota(jnp.int32, (length, half), 1)
    near = key <= me_c * half + lane
    far = key + length <= (2 * count_c - 1 - me_c) * half + lane
    return near, far


def attn_kernel(ids_ref, q_ref, kv_ref, gain_ref, cos_ref, sin_ref, attn_ref, lse_ref, qb_ref, q_nat, k_nat, v_nat):
    me_s, me_c = ids_ref[0], ids_ref[1]
    count_s, _, own, width = q_ref.shape
    count_c = kv_ref.shape[0]
    dim = gain_ref.shape[-1]
    rows = count_s * own
    half = rows // 2
    length = count_c * half
    scale = dim ** (-0.5)
    natural_rows(me_s, count_s, q_ref, q_nat)
    gather_keys(me_s, me_c, kv_ref, k_nat, v_nat)
    near, far = masks(me_c, count_c, half)
    v_t = v_nat[...].astype(F32).T.astype(BF)
    for h in range(width // dim):
        lanes = slice(h * dim, (h + 1) * dim)
        u = q_nat[:, lanes]
        q = turn(u * inv_rms(u) * gain_ref[...], cos_ref[...], sin_ref[...]).astype(BF)
        qb_ref[0, :, lanes] = q
        s_a = mm_nt(k_nat[:length], q) * scale
        s_n = jnp.where(near, s_a[:, :half], -1e30)
        s_f = s_a[:, half:]
        s_b = jnp.where(far, mm_nt(k_nat[length:], q[half:]) * scale, -1e30)
        m_n = jnp.max(s_n, 0, keepdims=True)
        m_f = jnp.maximum(jnp.max(s_f, 0, keepdims=True), jnp.max(s_b, 0, keepdims=True))
        e_n = jnp.exp(s_n - m_n)
        e_f = jnp.exp(s_f - m_f)
        e_b = jnp.exp(s_b - m_f)
        l_n = jnp.sum(e_n, 0, keepdims=True)
        l_f = jnp.sum(e_f, 0, keepdims=True) + jnp.sum(e_b, 0, keepdims=True)
        lse_ref[0, h : h + 1, :half] = m_n + jnp.log(l_n)
        lse_ref[0, h : h + 1, half:] = m_f + jnp.log(l_f)
        r_n, r_f = 1.0 / l_n, 1.0 / l_f
        o_n = mm(v_t[:, :length], (e_n * r_n).astype(BF))
        o_f = mm(v_t[:, :length], (e_f * r_f).astype(BF)) + mm(v_t[:, length:], (e_b * r_f).astype(BF))
        o = jnp.concatenate([o_n.T, o_f.T], 0).astype(BF)
        for j in range(count_s):
            attn_ref[me_s ^ j, 0, :, lanes] = o[j * own : (j + 1) * own]


def attn_grad_kernel(ids_ref, qb_ref, q_ref, kv_ref, do_ref, attn_ref, lse_ref, gain_ref, cos_ref, sin_ref, gq_ref, dkv_ref, gain_out, q_nat, k_nat, v_nat, do_nat, attn_nat, dk_acc, dv_acc):
    me_s, me_c = ids_ref[0], ids_ref[1]
    count_s, _, own, width = q_ref.shape
    count_c = kv_ref.shape[0]
    dim = gain_ref.shape[-1]
    rows = count_s * own
    half = rows // 2
    length = count_c * half
    scale = dim ** (-0.5)
    natural_rows(me_s, count_s, q_ref, q_nat)
    natural_rows(me_s, count_s, do_ref, do_nat)
    natural_rows(me_s, count_s, attn_ref, attn_nat)
    gather_keys(me_s, me_c, kv_ref, k_nat, v_nat)
    near, far = masks(me_c, count_c, half)
    k_t = k_nat[...].astype(F32).T.astype(BF)
    heads = width // dim
    lane = lax.broadcasted_iota(jnp.int32, (rows, dim), 1)
    delta = jnp.zeros((rows, dim), F32)
    for h in range(heads):
        lanes = slice(h * dim, (h + 1) * dim)
        both = jnp.sum(do_nat[:, lanes].astype(F32) * attn_nat[:, lanes].astype(F32), -1, keepdims=True)
        delta = jnp.where(lane == h, both, delta)
    delta_t = delta.T
    gain_total = jnp.zeros((1, dim), F32)
    for h in range(heads):
        lanes = slice(h * dim, (h + 1) * dim)
        q = qb_ref[0, :, lanes]
        do = do_nat[:, lanes]
        lse = lse_ref[0, h : h + 1, :]
        dlt = delta_t[h : h + 1, :]
        s_a = mm_nt(k_nat[:length], q) * scale
        dp_a = mm_nt(v_nat[:length], do)
        p_n = jnp.exp(jnp.where(near, s_a[:, :half], -1e30) - lse[:, :half])
        p_f = jnp.exp(s_a[:, half:] - lse[:, half:])
        p_a = jnp.concatenate([p_n, p_f], 1)
        ds_a = (p_a * (dp_a - dlt) * scale).astype(BF)
        p_a = p_a.astype(BF)
        s_b = jnp.where(far, mm_nt(k_nat[length:], q[half:]) * scale, -1e30)
        dp_b = mm_nt(v_nat[length:], do[half:])
        p_b = jnp.exp(s_b - lse[:, half:])
        ds_b = (p_b * (dp_b - dlt[:, half:]) * scale).astype(BF)
        p_b = p_b.astype(BF)
        dk_a, dv_a = mm(ds_a, q), mm(p_a, do)
        dk_b, dv_b = mm(ds_b, q[half:]), mm(p_b, do[half:])
        if h == 0:
            dk_acc[:length], dv_acc[:length] = dk_a, dv_a
            dk_acc[length:], dv_acc[length:] = dk_b, dv_b
        else:
            dk_acc[:length] += dk_a
            dv_acc[:length] += dv_a
            dk_acc[length:] += dk_b
            dv_acc[length:] += dv_b
        dq_a = mm(k_t[:, :length], ds_a)
        dq_f = dq_a[:, half:] + mm(k_t[:, length:], ds_b)
        dq = jnp.concatenate([dq_a[:, :half].T, dq_f.T], 0)
        grad = turn_back(dq, cos_ref[...], sin_ref[...])
        u = q_nat[:, lanes]
        inverse = inv_rms(u)
        hat = u * inverse
        gain_total = gain_total + jnp.sum(grad * hat, 0, keepdims=True)
        out = norm_backward_step(grad, hat, inverse, gain_ref[...]).astype(BF)
        for j in range(count_s):
            gq_ref[me_s ^ j, 0, :, lanes] = out[j * own : (j + 1) * own]
    gain_out[0] = gain_total
    for jc in range(count_c):
        for j in range(count_s):
            row = j * own
            at = jc * half + row if row < half else (2 * count_c - 1 - jc) * half + row - half
            dkv_ref[me_c ^ jc, 0, me_s ^ j, 0] = dk_acc[at : at + own, :].astype(BF)
            dkv_ref[me_c ^ jc, 1, me_s ^ j, 0] = dv_acc[at : at + own, :].astype(BF)


def expert_grad_kernel(rows_ref, grad_in_ref, grads_ref, inner_ref, out_ref):
    wide = grads_ref.shape[1]
    out_ref[:, :wide] = mm_tn(rows_ref[...], grads_ref[...]).astype(BF)
    out_ref[:, wide:] = mm_tn(grad_in_ref[...], inner_ref[...]).astype(BF)


def expert_grads(rows, grad_in, grads, inner):
    count, width = rows.shape
    tile = 256 if width % 256 == 0 else width
    wide = grads.shape[1] + inner.shape[1]

    def resident(value):
        return pl.BlockSpec(value.shape, lambda i: (0, 0))

    return pl.pallas_call(
        expert_grad_kernel,
        grid=(width // tile,),
        in_specs=[
            pl.BlockSpec((count, tile), lambda i: (0, i)),
            pl.BlockSpec((count, tile), lambda i: (0, i)),
            resident(grads),
            resident(inner),
        ],
        out_specs=pl.BlockSpec((tile, wide), lambda i: (i, 0)),
        out_shape=jax.ShapeDtypeStruct((width, wide), BF),
        name="expert_grads",
        cost_estimate=pl.CostEstimate(
            flops=2 * count * width * wide, bytes_accessed=4 * (count + wide) * width, transcendentals=0
        ),
    )(rows, grad_in, grads, inner)


def after(value, *others):
    return lax.optimization_barrier((value, *others))[0]


def per_device(
    tokens,
    gain_attn,
    gain_mlp,
    gain_query,
    key_norm_gain,
    w_query,
    key_matrix,
    value_matrix,
    w_out,
    w_gate,
    w_up,
    w_down,
    expert_ids,
    route_weight,
    cotangent,
):
    count_c = lax.axis_size("ctx")
    count_s = lax.axis_size("shard")
    me_c = lax.axis_index("ctx")
    me_s = lax.axis_index("shard")
    seqs, block_rows, width = tokens.shape
    own = expert_ids.shape[1]
    head_dim = gain_query.shape[0]
    q_width = w_query.shape[1]
    heads = q_width // head_dim
    hidden_width = w_gate.shape[2]
    half = block_rows // 2
    seq_len = block_rows * count_c
    own_rows = seqs * own
    all_rows = count_s * own_rows
    both = ("ctx", "dp")

    def gather(value):
        return lax.all_gather(value, both, axis=0, tiled=True)

    def scatter(value):
        return lax.psum_scatter(value, both, scatter_dimension=0, tiled=True)

    def sum_cores(value):
        count_d = lax.axis_size("dp")
        me_d = lax.axis_index("dp")
        parts = value.reshape(count_c, count_d, -1, value.shape[1])
        total = lax.dynamic_index_in_dim(parts, me_d, 1, False).astype(F32)
        for k in range(1, count_d):
            sent = lax.dynamic_index_in_dim(parts, me_d ^ k, 1, False)
            total = total + swap(sent, "dp", k).astype(F32)
        return total.astype(BF)

    def sum_ctx(total):
        result = lax.dynamic_index_in_dim(total, me_c, 0, False).astype(F32)
        for k in order_of(count_c):
            sent = lax.dynamic_index_in_dim(total, me_c ^ k, 0, False)
            result = result + swap(sent, "ctx", k).astype(F32)
        return result

    full_qkv = gather(jnp.concatenate([w_query, key_matrix, value_matrix], 1))
    full_out = gather(w_out)
    full_experts = gather(jnp.concatenate([w_gate[0], w_up[0], w_down[0]], 1))

    rows_at = [
        lax.dynamic_slice_in_dim(tokens, (me_s ^ k) * own, own, 1).reshape(own_rows, width)
        for k in range(count_s)
    ]
    residual = jnp.concatenate(rows_at, 0).astype(F32)
    inverse_one = inv_rms(residual)
    hat_one = residual * inverse_one
    normed_one = (hat_one * gain_attn).astype(BF)
    residual_own = rows_at[0].astype(F32)
    inverse_own = inv_rms(residual_own)
    hat_own = residual_own * inverse_own

    grad_top = cotangent.reshape(own_rows, width)
    grad_all = jnp.concatenate(collect(grad_top, "shard"), 0)
    ids = expert_ids.reshape(own_rows, -1)
    weights = route_weight.reshape(own_rows, -1)

    def weight_for(expert):
        return jnp.sum(jnp.where(ids == expert, weights, 0.0), -1)

    coefs = {0: weight_for(me_s)}
    for k in order_of(count_s):
        coefs[k] = swap(weight_for(me_s ^ k), "shard", k)
    coef = jnp.concatenate([coefs[k] for k in range(count_s)], 0)[:, None]
    grad_rows = (coef * grad_all.astype(F32)).astype(BF)

    block = jnp.arange(count_s, dtype=jnp.int32)
    offsets = jnp.arange(own, dtype=jnp.int32)
    row_natural = me_c * block_rows + jnp.arange(block_rows, dtype=jnp.int32)
    cos_nat, sin_nat = rope_tables(folded_positions(row_natural, count_c, half), head_dim)
    row_peer = me_c * block_rows + (me_s ^ block)[:, None] * own + offsets
    cos_peer, sin_peer = rope_tables(folded_positions(row_peer, count_c, half), head_dim)

    def spread(table):
        return jnp.broadcast_to(
            table[:, None], (count_s, seqs, own, head_dim)
        ).reshape(all_rows, head_dim)

    cos_rows, sin_rows = spread(cos_peer), spread(sin_peer)
    gain_q_row, gain_k_row = gain_query[None], key_norm_gain[None]

    normed_one = after(normed_one, grad_rows)
    kv_raw = mm(normed_one, full_qkv[:, q_width:])
    kv_own = pl.pallas_call(
        key_kernel, out_shape=jax.ShapeDtypeStruct((2, all_rows, head_dim), BF), name="key_prep"
    )(kv_raw, gain_k_row, cos_rows, sin_rows)
    kv_all = jnp.stack(collect(kv_own, "ctx"), 0).reshape(
        count_c, 2, count_s, seqs, own, head_dim
    )
    full_query = full_qkv[:, :q_width]
    queries = mm(normed_one, full_query).reshape(count_s, seqs, own, q_width)
    kv_weights = jnp.concatenate(collect(full_qkv[:, q_width:], "shard"), 1)

    me_ids = jnp.stack([me_s, me_c]).astype(jnp.int32)
    row_spec = pl.BlockSpec((count_s, 1, own, q_width), lambda s, _: (0, s, 0, 0))
    kv_spec = pl.BlockSpec(
        (count_c, 2, count_s, 1, own, head_dim), lambda s, _: (0, 0, 0, s, 0, 0)
    )
    nat_spec = pl.BlockSpec((1, block_rows, q_width), lambda s, _: (s, 0, 0))
    lse_spec = pl.BlockSpec((1, heads, block_rows), lambda s, _: (s, 0, 0))

    def whole(shape):
        return pl.BlockSpec(shape, lambda s, _: (0,) * len(shape))

    table_spec = whole((block_rows, head_dim))
    gain_spec = whole((1, head_dim))
    me_ids, kv_weights = lax.optimization_barrier((me_ids, kv_weights))
    attn, lse, queries_bf = pl.pallas_call(
        attn_kernel,
        grid_spec=pltpu.PrefetchScalarGridSpec(
            num_scalar_prefetch=1,
            grid=(seqs,),
            in_specs=[row_spec, kv_spec, gain_spec, table_spec, table_spec],
            out_specs=[row_spec, lse_spec, nat_spec],
            scratch_shapes=[
                pltpu.VMEM((block_rows, q_width), F32),
                pltpu.VMEM((seq_len, head_dim), BF),
                pltpu.VMEM((seq_len, head_dim), BF),
            ],
        ),
        out_shape=[
            jax.ShapeDtypeStruct((count_s, seqs, own, q_width), BF),
            jax.ShapeDtypeStruct((seqs, heads, block_rows), F32),
            jax.ShapeDtypeStruct((seqs, block_rows, q_width), BF),
        ],
        name="attn_fwd",
        cost_estimate=pl.CostEstimate(
            flops=4 * all_rows * seq_len * q_width, bytes_accessed=16 * all_rows * q_width, transcendentals=0
        ),
    )(me_ids, queries, kv_all, gain_q_row, cos_nat, sin_nat)

    def reduce_blocks(block_of):
        got = {}
        for k in order_of(count_s):
            got[k] = swap(block_of(k).astype(BF), "shard", k)
        total = block_of(0).astype(F32)
        for k in range(1, count_s):
            total = total + got[k].astype(F32)
        return total

    attended = reduce_blocks(lambda k: mm_nt(attn[k].reshape(own_rows, q_width), full_out))
    hidden = residual_own + attended
    inverse_two = inv_rms(hidden)
    hat_two = hidden * inverse_two
    normed_two = (hat_two * gain_mlp).astype(BF)
    arrived = jnp.concatenate(collect(normed_two, "shard"), 0)

    full_gate_up = full_experts[:, : 2 * hidden_width]
    full_down = full_experts[:, 2 * hidden_width :]
    grad_inner = mm(grad_rows, full_down)
    pre = mm(arrived, full_gate_up)
    gate_pre, up_pre = pre[:, :hidden_width], pre[:, hidden_width:]
    gate_sig = jax.nn.sigmoid(gate_pre)
    gate_act = gate_pre * gate_sig
    inner_bf = (gate_act * up_pre).astype(BF)
    grad_gate = grad_inner * up_pre * gate_sig * (1.0 + gate_pre * (1.0 - gate_sig))
    grad_up = grad_inner * gate_act
    grad_gate_up = jnp.concatenate([grad_gate.astype(BF), grad_up.astype(BF)], 1)
    grad_slots = mm_nt(grad_gate_up, full_gate_up)
    grad_normed_two = reduce_blocks(lambda k: grad_slots[k * own_rows : (k + 1) * own_rows])
    grad_w_experts = expert_grads(arrived, grad_rows, after(grad_gate_up, grad_slots), inner_bf)
    sum_experts = scatter(grad_w_experts).astype(F32)

    gain_mlp_part = jnp.sum(grad_normed_two * hat_two, 0)
    grad_hidden = grad_top.astype(F32) + norm_backward_step(
        grad_normed_two, hat_two, inverse_two, gain_mlp
    )
    expert_out = mm_nt(inner_bf, full_down).astype(BF).astype(F32)
    weighted = coef * expert_out
    weighted = weighted.astype(BF)
    route_part = jnp.sum(grad_all.astype(F32) * expert_out, -1)
    grad_hidden_bf = after(grad_hidden.astype(BF), grad_w_experts)
    grad_att = jnp.concatenate(collect(grad_hidden_bf, "shard"), 0)
    grad_att, weighted, route_part = lax.optimization_barrier((grad_att, weighted, route_part))
    mixture = reduce_blocks(lambda k: weighted[k * own_rows : (k + 1) * own_rows])
    block_out = (hidden + mixture).astype(BF)
    route_all = {0: route_part[:own_rows]}
    for k in order_of(count_s):
        route_all[k] = swap(route_part[k * own_rows : (k + 1) * own_rows], "shard", k)
    route_grad = jnp.zeros(ids.shape, F32)
    for k in range(count_s):
        route_grad = jnp.where(ids == (me_s ^ k), route_all[k][:, None], route_grad)

    attention_gradient = mm(grad_att, full_out).astype(BF)

    grad_q, grad_kv, gain_q_parts = pl.pallas_call(
        attn_grad_kernel,
        grid_spec=pltpu.PrefetchScalarGridSpec(
            num_scalar_prefetch=1,
            grid=(seqs,),
            in_specs=[
                nat_spec, row_spec, kv_spec, row_spec, row_spec, lse_spec,
                gain_spec, table_spec, table_spec,
            ],
            out_specs=[row_spec, kv_spec, pl.BlockSpec((1, 1, head_dim), lambda s, _: (s, 0, 0))],
            scratch_shapes=[
                pltpu.VMEM((block_rows, q_width), F32),
                pltpu.VMEM((seq_len, head_dim), BF),
                pltpu.VMEM((seq_len, head_dim), BF),
                pltpu.VMEM((block_rows, q_width), BF),
                pltpu.VMEM((block_rows, q_width), BF),
                pltpu.VMEM((seq_len, head_dim), F32),
                pltpu.VMEM((seq_len, head_dim), F32),
            ],
        ),
        out_shape=[
            jax.ShapeDtypeStruct((count_s, seqs, own, q_width), BF),
            jax.ShapeDtypeStruct((count_c, 2, count_s, seqs, own, head_dim), BF),
            jax.ShapeDtypeStruct((seqs, 1, head_dim), F32),
        ],
        name="attn_bwd",
        cost_estimate=pl.CostEstimate(
            flops=10 * all_rows * seq_len * q_width, bytes_accessed=32 * all_rows * q_width, transcendentals=0
        ),
    )(
        me_ids, queries_bf, queries, kv_all,
        attention_gradient.reshape(count_s, seqs, own, q_width),
        attn, lse, gain_q_row, cos_nat, sin_nat,
    )
    grad_kv = grad_kv.reshape(count_c, 2, all_rows, head_dim)
    grad_q = grad_q.reshape(all_rows, q_width)
    grad_w_query = mm_tn(normed_one, grad_q).astype(BF)
    sum_query = scatter(grad_w_query).astype(F32)
    query_part = reduce_blocks(
        lambda k: mm_nt(grad_q[k * own_rows : (k + 1) * own_rows], full_query)
    )
    grad_w_out = mm_tn(after(grad_att, grad_kv), attn.reshape(all_rows, q_width)).astype(BF)
    half_sum_out = sum_cores(grad_w_out)
    sum_out = sum_ctx(half_sum_out)

    kv_parts = [grad_kv[0]]
    for k in range(1, count_c):
        kv_parts.append(swap(grad_kv[k], "ctx", k))
    kv_parts = list(lax.optimization_barrier((*kv_parts, half_sum_out))[:count_c])
    grad_kv_bf, gain_k_part = pl.pallas_call(
        functools.partial(key_grad_kernel, count_c),
        out_shape=[
            jax.ShapeDtypeStruct((all_rows, 2 * head_dim), BF),
            jax.ShapeDtypeStruct((1, head_dim), F32),
        ],
        name="key_grad",
    )(kv_raw, gain_k_row, cos_rows, sin_rows, *kv_parts)
    kv_rows = {
        k: swap(grad_kv_bf[k * own_rows : (k + 1) * own_rows], "shard", k)
        for k in order_of(count_s)
    }
    kv_rows[0] = grad_kv_bf[:own_rows]
    sum_kv = sum_ctx(sum_cores(mm_tn(normed_one, grad_kv_bf).astype(BF)))
    grad_normed_one = query_part + mm_nt(
        jnp.concatenate([kv_rows[k] for k in range(count_s)], 1), kv_weights
    )
    gain_attn_part = jnp.sum(grad_normed_one * hat_own, 0)
    grad_tokens = grad_hidden + norm_backward_step(
        grad_normed_one, hat_own, inverse_own, gain_attn
    )
    gains = jnp.concatenate(
        [gain_attn_part, gain_mlp_part, jnp.sum(gain_q_parts, (0, 1)), gain_k_part[0]]
    ).reshape(-1, head_dim)
    for axis in ("dp", "shard", "ctx"):
        step = 1
        while step < lax.axis_size(axis):
            gains = gains + swap(gains, axis, step)
            step *= 2
    gains = gains.reshape(-1)

    def own_shape(value):
        return value.reshape(seqs, own, value.shape[-1])

    return (
        own_shape(block_out),
        own_shape(grad_tokens),
        lse,
        own_shape(route_grad),
        gains[:width],
        gains[width : 2 * width],
        gains[2 * width : 2 * width + head_dim],
        gains[2 * width + head_dim :],
        sum_query,
        sum_kv[:, :head_dim],
        sum_kv[:, head_dim:],
        sum_out,
        sum_experts[None, :, :hidden_width],
        sum_experts[None, :, hidden_width : 2 * hidden_width],
        sum_experts[None, :, 2 * hidden_width :],
    )


def solution(mesh):
    placed = (
        P("dp", "ctx", None),
        P(),
        P(),
        P(),
        P(),
        P(("ctx", "dp"), "shard"),
        P(("ctx", "dp"), "shard"),
        P(("ctx", "dp"), "shard"),
        P(("ctx", "dp"), "shard"),
        P("shard", ("ctx", "dp"), None),
        P("shard", ("ctx", "dp"), None),
        P("shard", ("ctx", "dp"), None),
        P("dp", ("ctx", "shard"), None),
        P("dp", ("ctx", "shard"), None),
        P("dp", ("ctx", "shard"), None),
    )

    return jax.shard_map(
        per_device,
        mesh=mesh,
        in_specs=placed,
        out_specs=(
            P("dp", ("ctx", "shard"), None),
            P("dp", ("ctx", "shard"), None),
            P("dp", "shard", "ctx"),
            P("dp", ("ctx", "shard"), None),
            P(),
            P(),
            P(),
            P(),
            P(("ctx", "dp"), "shard"),
            P(("ctx", "dp"), "shard"),
            P(("ctx", "dp"), "shard"),
            P(("ctx", "dp"), "shard"),
            P("shard", ("ctx", "dp"), None),
            P("shard", ("ctx", "dp"), None),
            P("shard", ("ctx", "dp"), None),
        ),
        check_vma=False,
    )
```

profile of v0, /device:TPU:0, one launch (start us, length us, event | category | flops | bytes accessed | tf_op | source)
XLA Modules:
  0.0 637.4 jit_solution(11153488813939653566)
XLA Ops:
  26.1 6.3 fusion.2
  32.6 18.5 %collective-permute-done.4 = f32[192]{0:T(256)S(1)} collective-permute-done((f32[192]{0:T(256)S(1)}, f32[192]{0:T(256)S(1)}, u32[]{:S(2)}, u32[]{:S(2)}) %collective-permute-start.4) | collective-permute-done | bytes 800 | tf_op jit(solution)/shard_map/ppermute | solution.py:22
  58.0 11.0 %all-gather.4.cloned.1.call-done = bf16[2048,1280]{1,0:T(8,128)(2,1)} async-done(((bf16[256,1280]{1,0:T(8,128)(2,1)}), bf16[2048,1280]{1,0:T(8,128)(2,1)}) %all-gather.4.cloned.1.call-update) | async-done | bytes 5242896 | tf_op jit(solution)/shard_map/all_gather | solution.py:312
  85.3 14.1 %collective-permute-done.11 = bf16[2,768,128]{2,1,0:T(8,128)(2,1)S(1)} collective-permute-done((bf16[2,768,128]{2,1,0:T(8,128)(2,1)}, bf16[2,768,128]{2,1,0:T(8,128)(2,1)S(1)}, u32[]{:S(2)}, u32[]{:S(2)}) %collective-permute-start.11) | collective-permute-done | bytes 393248 | tf_op jit(solution)/shard_map/ppermute | solution.py:22
  99.3 26.7 %collective-permute-start.9 = (bf16[2,768,128]{2,1,0:T(8,128)(2,1)}, bf16[2,768,128]{2,1,0:T(8,128)(2,1)S(1)}, u32[]{:S(2)}, u32[]{:S(2)}) collective-permute-start(bf16[2,768,128]{2,1,0:T(8,128)(2,1)} %key_prep.1), channel_id=1, source_target_pairs={{0,8},{8,0},{16,24},{24,16},{1,9},{9,1},{17,25},{25,17},{2,10},{10... | collective-permute-start | bytes 1179656 | tf_op jit(solution)/shard_map/ppermute | solution.py:22
  126.0 7.3 %fusion.20 = f32[768,1024]{1,0:T(8,128)} fusion(bf16[768,2048]{1,0:T(8,128)(2,1)S(1)} %copy-done.10, bf16[2048,1280]{1,0:T(8,128)(2,1)} %all-gather.4.cloned.1.call-done), kind=kOutput, calls=%fused_computation.46 | convolution fusion | flops 3221225472 | bytes 10485760 | tf_op jit(solution)/shard_map/dot_general | solution.py:63
  133.3 12.7 %collective-permute-done.10 = bf16[2,768,128]{2,1,0:T(8,128)(2,1)S(1)} collective-permute-done((bf16[2,768,128]{2,1,0:T(8,128)(2,1)}, bf16[2,768,128]{2,1,0:T(8,128)(2,1)S(1)}, u32[]{:S(2)}, u32[]{:S(2)}) %collective-permute-start.10) | collective-permute-done | bytes 393248 | tf_op jit(solution)/shard_map/ppermute | solution.py:22
  146.0 5.3 collective-permute-done.9
  154.9 17.6 %attn_fwd.1 = (bf16[4,3,64,1024]{3,2,1,0:T(8,128)(2,1)}, f32[3,8,256]{2,1,0:T(8,128)}, bf16[3,256,1024]{2,1,0:T(8,128)(2,1)}) custom-call(s32[2]{0:T(128)} %pad_add_fusion.ids_ref, f32[4,3,64,1024]{3,2,1,0:T(8,128)} %bitcast.176, bf16[4,2,4,3,64,128]{5,4,3,2,1,0:T(8,128)(2,1)} %pad_maximum_fusion.6.kv_ref, f32[1,128]{1,0:T(1,128)} %bitcast.174, ...), custom_call_target="tpu_custom_call" | custom-call | flops 3221225472 | bytes 12582912 | tf_op jit(solution)/shard_map/attn_fwd/pallas_call | solution.py:405
  184.7 11.9 %collective-permute-done.13 = bf16[192,2048]{1,0:T(8,128)(2,1)S(1)} collective-permute-done((bf16[192,2048]{1,0:T(8,128)(2,1)S(1)}, bf16[192,2048]{1,0:T(8,128)(2,1)S(1)}, u32[]{:S(2)}, u32[]{:S(2)}) %collective-permute-start.13) | collective-permute-done | bytes 786464 | tf_op jit(solution)/shard_map/ppermute | solution.py:22
  196.6 4.8 collective-permute-done.12
  201.5 14.8 %collective-permute-done.14 = bf16[192,2048]{1,0:T(8,128)(2,1)S(1)} collective-permute-done((bf16[192,2048]{1,0:T(8,128)(2,1)S(1)}, bf16[192,2048]{1,0:T(8,128)(2,1)S(1)}, u32[]{:S(2)}, u32[]{:S(2)}) %collective-permute-start.14) | collective-permute-done | bytes 786464 | tf_op jit(solution)/shard_map/ppermute | solution.py:22
  222.0 17.9 %collective-permute-done.17 = bf16[192,2048]{1,0:T(8,128)(2,1)S(1)} collective-permute-done((bf16[192,2048]{1,0:T(8,128)(2,1)S(1)}, bf16[192,2048]{1,0:T(8,128)(2,1)S(1)}, u32[]{:S(2)}, u32[]{:S(2)}) %collective-permute-start.17) | collective-permute-done | bytes 786464 | tf_op jit(solution)/shard_map/ppermute | solution.py:22
  239.9 14.2 %collective-permute-done.16 = bf16[192,2048]{1,0:T(8,128)(2,1)S(1)} collective-permute-done((bf16[192,2048]{1,0:T(8,128)(2,1)S(1)}, bf16[192,2048]{1,0:T(8,128)(2,1)S(1)}, u32[]{:S(2)}, u32[]{:S(2)}) %collective-permute-start.16) | collective-permute-done | bytes 786464 | tf_op jit(solution)/shard_map/ppermute | solution.py:22
  257.7 9.9 %fusion.8 = f32[768,1536]{1,0:T(8,128)S(1)} fusion(bf16[2048,2304]{1,0:T(8,128)(2,1)} %all-gather.8.cloned.1.call-done, bf16[192,2048]{1,0:T(8,128)(2,1)} %copy-done.16, bf16[192,2048]{1,0:T(8,128)(2,1)} %copy-done.17, bf16[192,2048]{1,0:T(8,128)(2,1)} %copy-done.18, bf16[192,2048]{1,0:T(8,128)(2,1)} %copy-done.9), kind=kOutput, calls=%fused_computation.13 | convolution fusion | flops 4844421120 | bytes 14155776 | tf_op jit(solution)/shard_map/dot_general | solution.py:63
  272.0 7.0 %fusion.73 = (bf16[768,2048]{1,0:T(8,128)(2,1)S(1)}, f32[768,2048]{1,0:T(8,128)}) fusion(bf16[2048,2304]{1,0:T(8,128)(2,1)S(1)} %copy-done.38, bf16[768,768]{1,0:T(8,128)(2,1)S(1)} %get-tuple-element.69, bf16[768,768]{1,0:T(8,128)(2,1)S(1)} %get-tuple-element.68), kind=kOutput, calls=%fused_computation.185 | convolution fusion | flops 4838129664 | bytes 18087936 | tf_op jit(solution)/shard_map/dot_general | solution.py:67
  285.6 13.9 %expert_grads.1 = bf16[2048,2304]{1,0:T(8,128)(2,1)} custom-call(bf16[768,2048]{1,0:T(8,128)(2,1)} %pad_maximum_fusion.3.rows_ref, bf16[768,2048]{1,0:T(8,128)(2,1)} %fusion.3.grad_in_ref, bf16[768,1536]{1,0:T(8,128)(2,1)} %pad_maximum_fusion.5.grads_ref, bf16[768,768]{1,0:T(8,128)(2,1)} %get-tuple-element.70.inner_ref), custom_call_target="tpu_custom_call" | custom-call | flops 7247757312 | bytes 25165824 | tf_op jit(solution)/shard_map/expert_grads/pallas_call | solution.py:256
  301.2 17.2 %collective-permute-done.20 = bf16[192,2048]{1,0:T(8,128)(2,1)} collective-permute-done((bf16[192,2048]{1,0:T(8,128)(2,1)}, bf16[192,2048]{1,0:T(8,128)(2,1)}, u32[]{:S(2)}, u32[]{:S(2)}) %collective-permute-start.20) | collective-permute-done | bytes 786464 | tf_op jit(solution)/shard_map/ppermute | solution.py:22
  327.9 7.4 %fusion.5 = (f32[768]{0:T(1024)S(1)}, bf16[768,2048]{1,0:T(8,128)(2,1)}) fusion(bf16[192,2048]{1,0:T(8,128)(2,1)} %collective-permute-done.8, bf16[192,2048]{1,0:T(8,128)(2,1)} %collective-permute-done.7, bf16[192,2048]{1,0:T(8,128)(2,1)} %collective-permute-done.6, bf16[192,2048]{1,0:T(8,128)(2,1)S(1)} %bitcast.137, f32[768]{0:T(1024)S(1)} %copy-done.26, ...), kind=kOutput, calls=%fused_computation.10 | convolution fusion | flops 2437938432 | bytes 10622976 | tf_op jit(solution)/shard_map/dot_general | solution.py:67
  335.4 10.4 %collective-permute-done.23 = bf16[192,2048]{1,0:T(8,128)(2,1)S(1)} collective-permute-done((bf16[192,2048]{1,0:T(8,128)(2,1)S(1)}, bf16[192,2048]{1,0:T(8,128)(2,1)S(1)}, u32[]{:S(2)}, u32[]{:S(2)}) %collective-permute-start.23) | collective-permute-done | bytes 786464 | tf_op jit(solution)/shard_map/ppermute | solution.py:22
  345.7 13.6 %collective-permute-done.22 = bf16[192,2048]{1,0:T(8,128)(2,1)S(1)} collective-permute-done((bf16[192,2048]{1,0:T(8,128)(2,1)S(1)}, bf16[192,2048]{1,0:T(8,128)(2,1)S(1)}, u32[]{:S(2)}, u32[]{:S(2)}) %collective-permute-start.22) | collective-permute-done | bytes 786464 | tf_op jit(solution)/shard_map/ppermute | solution.py:22
  364.4 19.3 %attn_bwd.1 = (bf16[4,3,64,1024]{3,2,1,0:T(8,128)(2,1)}, bf16[4,2,4,3,64,128]{5,4,3,2,1,0:T(8,128)(2,1)}, f32[3,1,128]{2,1,0:T(1,128)}) custom-call(s32[2]{0:T(128)} %pad_add_fusion.ids_ref, bf16[3,256,1024]{2,1,0:T(8,128)(2,1)} %get-tuple-element.41.qb_ref, f32[4,3,64,1024]{3,2,1,0:T(8,128)} %bitcast.177, ...), custom_call_target="tpu_custom_call" | custom-call | flops 8053063680 | bytes 25165824 | tf_op jit(solution)/shard_map/attn_bwd/pallas_call | solution.py:483
  383.8 7.9 %convolution_convert_fusion = bf16[2048,1024]{1,0:T(8,128)(2,1)} fusion(bf16[768,2048]{1,0:T(8,128)(2,1)} %fusion.2, bf16[768,1024]{1,0:T(8,128)(2,1)} %bitcast.146), kind=kOutput, calls=%fused_computation.18 | convolution fusion | flops 3223322624 | bytes 8912896 | tf_op jit(solution)/shard_map/dot_general | solution.py:71
  401.7 5.3 convolution_convert_fusion.1
  410.2 5.5 convolution_convert_fusion.4
  434.3 11.6 %collective-permute-done.31.refs_2_ = bf16[2,768,128]{2,1,0:T(8,128)(2,1)} collective-permute-done((bf16[2,768,128]{2,1,0:T(8,128)(2,1)}, bf16[2,768,128]{2,1,0:T(8,128)(2,1)}, u32[]{:S(2)}, u32[]{:S(2)}) %collective-permute-start.31) | collective-permute-done | bytes 393248 | tf_op jit(solution)/shard_map/ppermute | solution.py:22
  452.3 6.8 %collective-permute-done.30.refs_1_ = bf16[2,768,128]{2,1,0:T(8,128)(2,1)} collective-permute-done((bf16[2,768,128]{2,1,0:T(8,128)(2,1)S(1)}, bf16[2,768,128]{2,1,0:T(8,128)(2,1)}, u32[]{:S(2)}, u32[]{:S(2)}) %collective-permute-start.30) | collective-permute-done | bytes 393248 | tf_op jit(solution)/shard_map/ppermute | solution.py:22
  468.2 15.1 %collective-permute-done.29 = bf16[192,2048]{1,0:T(8,128)(2,1)} collective-permute-done((bf16[192,2048]{1,0:T(8,128)(2,1)}, bf16[192,2048]{1,0:T(8,128)(2,1)}, u32[]{:S(2)}, u32[]{:S(2)}) %collective-permute-start.29) | collective-permute-done | bytes 786464 | tf_op jit(solution)/shard_map/ppermute | solution.py:22
  487.6 5.6 fusion.29
  495.3 24.2 %collective-permute-done.41 = f32[34,128]{1,0:T(8,128)S(1)} collective-permute-done((f32[34,128]{1,0:T(8,128)S(1)}, f32[34,128]{1,0:T(8,128)S(1)}, u32[]{:S(2)}, u32[]{:S(2)}) %collective-permute-start.41) | collective-permute-done | bytes 17440 | tf_op jit(solution)/shard_map/ppermute | solution.py:22
  538.0 71.1 %collective-permute-done.44 = f32[34,128]{1,0:T(8,128)S(1)} collective-permute-done((f32[34,128]{1,0:T(8,128)S(1)}, f32[34,128]{1,0:T(8,128)S(1)}, u32[]{:S(2)}, u32[]{:S(2)}) %collective-permute-start.44) | collective-permute-done | bytes 17440 | tf_op jit(solution)/shard_map/ppermute | solution.py:22
  617.7 7.0 %collective-permute-done.48 = bf16[256,256]{1,0:T(8,128)(2,1)S(1)} collective-permute-done((bf16[256,256]{1,0:T(8,128)(2,1)S(1)}, bf16[256,256]{1,0:T(8,128)(2,1)S(1)}, u32[]{:S(2)}, u32[]{:S(2)}) %collective-permute-start.48) | collective-permute-done | bytes 131104 | tf_op jit(solution)/shard_map/ppermute | solution.py:22
  (269 shorter events, 180.7 us)
Async XLA Ops:
  7.2 61.8 %all-gather.4.cloned.1.call-start = ((), (), s32[]{:S(2)}) async-start(), calls=%async_computation.2 | async-start | bytes 5898240 | tf_op jit(solution)/shard_map/all_gather | solution.py:312
  9.3 164.7 %all-gather.6.cloned.1.call-start = ((), (), s32[]{:S(2)}) async-start(), calls=%async_computation.3 | async-start | bytes 4718592 | tf_op jit(solution)/shard_map/all_gather | solution.py:312
  10.1 247.6 %all-gather.8.cloned.1.call-start = ((), (), s32[]{:S(2)}) async-start(), calls=%async_computation.4 | async-start | bytes 10616832 | tf_op jit(solution)/shard_map/all_gather | solution.py:312
  12.5 613.1 %reduce-scatter.3.cloned.1.call-start = ((), (), s32[]{:S(2)}) async-start(), calls=%async_computation.5 | async-start | bytes 4718592 | tf_op jit(solution)/shard_map/reduce_scatter | solution.py:315
  12.5 42.2 %collective-permute-start.8 = (bf16[192,2048]{1,0:T(8,128)(2,1)S(1)}, bf16[192,2048]{1,0:T(8,128)(2,1)}, u32[]{:S(2)}, u32[]{:S(2)}) collective-permute-start(bf16[192,2048]{1,0:T(8,128)(2,1)S(1)} %bitcast.133), channel_id=1, source_target_pairs={{0,6},{2,4},{4,2},{6,0},{1,7},{3,5},{5,3},{7,1},{8,14},{10,12},{12... | collective-permute-start | bytes 2359304 | tf_op jit(solution)/shard_map/ppermute | solution.py:22
  16.5 38.2 %collective-permute-start.7 = (bf16[192,2048]{1,0:T(8,128)(2,1)S(1)}, bf16[192,2048]{1,0:T(8,128)(2,1)}, u32[]{:S(2)}, u32[]{:S(2)}) collective-permute-start(bf16[192,2048]{1,0:T(8,128)(2,1)S(1)} %bitcast.134), channel_id=1, source_target_pairs={{0,4},{2,6},{4,0},{6,2},{1,5},{3,7},{5,1},{7,3},{8,12},{10,14},{12... | collective-permute-start | bytes 2359304 | tf_op jit(solution)/shard_map/ppermute | solution.py:22
  17.0 37.7 %collective-permute-start.6 = (bf16[192,2048]{1,0:T(8,128)(2,1)S(1)}, bf16[192,2048]{1,0:T(8,128)(2,1)}, u32[]{:S(2)}, u32[]{:S(2)}) collective-permute-start(bf16[192,2048]{1,0:T(8,128)(2,1)S(1)} %bitcast.135), channel_id=1, source_target_pairs={{0,2},{2,0},{4,6},{6,4},{1,3},{3,1},{5,7},{7,5},{8,10},{10,8},{12,... | collective-permute-start | bytes 2359304 | tf_op jit(solution)/shard_map/ppermute | solution.py:22
  17.3 33.8 %collective-permute-start.4 = (f32[192]{0:T(256)S(1)}, f32[192]{0:T(256)S(1)}, u32[]{:S(2)}, u32[]{:S(2)}) collective-permute-start(f32[192]{0:T(256)S(1)} %reduce_sum.131), channel_id=1, source_target_pairs={{0,4},{2,6},{4,0},{6,2},{1,5},{3,7},{5,1},{7,3},{8,12},{10,14},{12... | collective-permute-start | bytes 2312 | tf_op jit(solution)/shard_map/ppermute | solution.py:22
  19.3 33.5 %collective-permute-start.5 = (f32[192]{0:T(256)S(1)}, f32[192]{0:T(256)S(1)}, u32[]{:S(2)}, u32[]{:S(2)}) collective-permute-start(f32[192]{0:T(256)S(1)} %reduce_sum.133), channel_id=1, source_target_pairs={{0,6},{2,4},{4,2},{6,0},{1,7},{3,5},{5,3},{7,1},{8,14},{10,12},{12... | collective-permute-start | bytes 2312 | tf_op jit(solution)/shard_map/ppermute | solution.py:22
  80.5 72.1 %collective-permute-start.2 = (bf16[2048,256]{1,0:T(8,128)(2,1)S(1)}, bf16[2048,256]{1,0:T(8,128)(2,1)S(1)}, u32[]{:S(2)}, u32[]{:S(2)}) collective-permute-start(bf16[2048,256]{1,0:T(8,128)(2,1)S(1)} %slice.218), channel_id=1, source_target_pairs={{0,6},{2,4},{4,2},{6,0},{1,7},{3,5},{5,3},{7,1},{8,14},{10,12},{12... | collective-permute-start | bytes 3145736 | tf_op jit(solution)/shard_map/ppermute | solution.py:22
  83.2 69.5 %collective-permute-start.1 = (bf16[2048,256]{1,0:T(8,128)(2,1)S(1)}, bf16[2048,256]{1,0:T(8,128)(2,1)S(1)}, u32[]{:S(2)}, u32[]{:S(2)}) collective-permute-start(bf16[2048,256]{1,0:T(8,128)(2,1)S(1)} %slice.218), channel_id=1, source_target_pairs={{0,4},{2,6},{4,0},{6,2},{1,5},{3,7},{5,1},{7,3},{8,12},{10,14},{12... | collective-permute-start | bytes 3145736 | tf_op jit(solution)/shard_map/ppermute | solution.py:22
  83.7 68.9 %collective-permute-start = (bf16[2048,256]{1,0:T(8,128)(2,1)S(1)}, bf16[2048,256]{1,0:T(8,128)(2,1)S(1)}, u32[]{:S(2)}, u32[]{:S(2)}) collective-permute-start(bf16[2048,256]{1,0:T(8,128)(2,1)S(1)} %slice.218), channel_id=1, source_target_pairs={{0,2},{2,0},{4,6},{6,4},{1,3},{3,1},{5,7},{7,5},{8,10},{10,8},{12,... | collective-permute-start | bytes 3145736 | tf_op jit(solution)/shard_map/ppermute | solution.py:22
  84.7 61.3 %collective-permute-start.10 = (bf16[2,768,128]{2,1,0:T(8,128)(2,1)}, bf16[2,768,128]{2,1,0:T(8,128)(2,1)S(1)}, u32[]{:S(2)}, u32[]{:S(2)}) collective-permute-start(bf16[2,768,128]{2,1,0:T(8,128)(2,1)} %key_prep.1), channel_id=1, source_target_pairs={{0,16},{8,24},{16,0},{24,8},{1,17},{9,25},{17,1},{25,9},{2,18},{10... | collective-permute-start | bytes 1179656 | tf_op jit(solution)/shard_map/ppermute | solution.py:22
  99.3 52.0 %collective-permute-start.9 = (bf16[2,768,128]{2,1,0:T(8,128)(2,1)}, bf16[2,768,128]{2,1,0:T(8,128)(2,1)S(1)}, u32[]{:S(2)}, u32[]{:S(2)}) collective-permute-start(bf16[2,768,128]{2,1,0:T(8,128)(2,1)} %key_prep.1), channel_id=1, source_target_pairs={{0,8},{8,0},{16,24},{24,16},{1,9},{9,1},{17,25},{25,17},{2,10},{10... | collective-permute-start | bytes 1179656 | tf_op jit(solution)/shard_map/ppermute | solution.py:22
  282.2 36.2 %collective-permute-start.20 = (bf16[192,2048]{1,0:T(8,128)(2,1)}, bf16[192,2048]{1,0:T(8,128)(2,1)}, u32[]{:S(2)}, u32[]{:S(2)}) collective-permute-start(bf16[192,2048]{1,0:T(8,128)(2,1)} %get-tuple-element.77), channel_id=1, source_target_pairs={{0,6},{2,4},{4,2},{6,0},{1,7},{3,5},{5,3},{7,1},{8,14},{10,12},{12... | collective-permute-start | bytes 2359304 | tf_op jit(solution)/shard_map/ppermute | solution.py:22
  283.7 36.1 %collective-permute-start.19 = (bf16[192,2048]{1,0:T(8,128)(2,1)}, bf16[192,2048]{1,0:T(8,128)(2,1)}, u32[]{:S(2)}, u32[]{:S(2)}) collective-permute-start(bf16[192,2048]{1,0:T(8,128)(2,1)} %get-tuple-element.78), channel_id=1, source_target_pairs={{0,4},{2,6},{4,0},{6,2},{1,5},{3,7},{5,1},{7,3},{8,12},{10,14},{12... | collective-permute-start | bytes 2359304 | tf_op jit(solution)/shard_map/ppermute | solution.py:22
  325.9 33.5 %collective-permute-start.22 = (bf16[192,2048]{1,0:T(8,128)(2,1)S(1)}, bf16[192,2048]{1,0:T(8,128)(2,1)S(1)}, u32[]{:S(2)}, u32[]{:S(2)}) collective-permute-start(bf16[192,2048]{1,0:T(8,128)(2,1)S(1)} %fusion.63), channel_id=1, source_target_pairs={{0,4},{2,6},{4,0},{6,2},{1,5},{3,7},{5,1},{7,3},{8,12},{10,14},{12... | collective-permute-start | bytes 2359304 | tf_op jit(solution)/shard_map/ppermute | solution.py:22
  326.2 33.2 %collective-permute-start.21 = (bf16[192,2048]{1,0:T(8,128)(2,1)S(1)}, bf16[192,2048]{1,0:T(8,128)(2,1)S(1)}, u32[]{:S(2)}, u32[]{:S(2)}) collective-permute-start(bf16[192,2048]{1,0:T(8,128)(2,1)S(1)} %fusion.63), channel_id=1, source_target_pairs={{0,2},{2,0},{4,6},{6,4},{1,3},{3,1},{5,7},{7,5},{8,10},{10,8},{12,... | collective-permute-start | bytes 2359304 | tf_op jit(solution)/shard_map/ppermute | solution.py:22
  391.7 236.0 %reduce-scatter.5.cloned.1.call-start = ((), (), s32[]{:S(2)}) async-start(), calls=%async_computation.6 | async-start | bytes 10616832 | tf_op jit(solution)/shard_map/reduce_scatter | solution.py:315
  399.4 46.5 %collective-permute-start.31 = (bf16[2,768,128]{2,1,0:T(8,128)(2,1)}, bf16[2,768,128]{2,1,0:T(8,128)(2,1)}, u32[]{:S(2)}, u32[]{:S(2)}) collective-permute-start(bf16[2,768,128]{2,1,0:T(8,128)(2,1)} %bitcast.31), channel_id=1, source_target_pairs={{0,16},{8,24},{16,0},{24,8},{1,17},{9,25},{17,1},{25,9},{2,18},{10... | collective-permute-start | bytes 1179656 | tf_op jit(solution)/shard_map/ppermute | solution.py:22
  408.6 37.6 %collective-permute-start.33 = (bf16[4,256,1024]{2,1,0:T(8,128)(2,1)}, bf16[4,256,1024]{2,1,0:T(8,128)(2,1)}, u32[]{:S(2)}, u32[]{:S(2)}) collective-permute-start(bf16[4,256,1024]{2,1,0:T(8,128)(2,1)} %dynamic-slice_bitcast_fusion), channel_id=1, source_target_pairs={{0,1},{1,0},{2,3},{3,2},{4,5},{5,4},{6,7},{7,6},{8,9},{9,8},{10,11... | collective-permute-start | bytes 6291464 | tf_op jit(solution)/shard_map/ppermute | solution.py:22
  423.9 35.2 %collective-permute-start.30 = (bf16[2,768,128]{2,1,0:T(8,128)(2,1)S(1)}, bf16[2,768,128]{2,1,0:T(8,128)(2,1)}, u32[]{:S(2)}, u32[]{:S(2)}) collective-permute-start(bf16[2,768,128]{2,1,0:T(8,128)(2,1)S(1)} %bitcast.159), channel_id=1, source_target_pairs={{0,8},{8,0},{16,24},{24,16},{1,9},{9,1},{17,25},{25,17},{2,10},{10... | collective-permute-start | bytes 1179656 | tf_op jit(solution)/shard_map/ppermute | solution.py:22
  424.6 39.8 %collective-permute-start.28 = (bf16[192,2048]{1,0:T(8,128)(2,1)}, bf16[192,2048]{1,0:T(8,128)(2,1)}, u32[]{:S(2)}, u32[]{:S(2)}) collective-permute-start(bf16[192,2048]{1,0:T(8,128)(2,1)} %convolution_convert_fusion.5), channel_id=1, source_target_pairs={{0,4},{2,6},{4,0},{6,2},{1,5},{3,7},{5,1},{7,3},{8,12},{10,14},{12... | collective-permute-start | bytes 2359304 | tf_op jit(solution)/shard_map/ppermute | solution.py:22
  446.2 37.0 %collective-permute-start.29 = (bf16[192,2048]{1,0:T(8,128)(2,1)}, bf16[192,2048]{1,0:T(8,128)(2,1)}, u32[]{:S(2)}, u32[]{:S(2)}) collective-permute-start(bf16[192,2048]{1,0:T(8,128)(2,1)} %convolution_convert_fusion.4), channel_id=1, source_target_pairs={{0,6},{2,4},{4,2},{6,0},{1,7},{3,5},{5,3},{7,1},{8,14},{10,12},{12... | collective-permute-start | bytes 2359304 | tf_op jit(solution)/shard_map/ppermute | solution.py:22
  468.2 62.4 %collective-permute-start.24 = (bf16[192,2048]{1,0:T(8,128)(2,1)}, bf16[192,2048]{1,0:T(8,128)(2,1)S(1)}, u32[]{:S(2)}, u32[]{:S(2)}) collective-permute-start(bf16[192,2048]{1,0:T(8,128)(2,1)} %get-tuple-element.71), channel_id=1, source_target_pairs={{0,2},{2,0},{4,6},{6,4},{1,3},{3,1},{5,7},{7,5},{8,10},{10,8},{12,... | collective-permute-start | bytes 2359304 | tf_op jit(solution)/shard_map/ppermute | solution.py:22
  483.3 47.4 %collective-permute-start.26 = (bf16[192,2048]{1,0:T(8,128)(2,1)}, bf16[192,2048]{1,0:T(8,128)(2,1)S(1)}, u32[]{:S(2)}, u32[]{:S(2)}) collective-permute-start(bf16[192,2048]{1,0:T(8,128)(2,1)} %get-tuple-element.72), channel_id=1, source_target_pairs={{0,6},{2,4},{4,2},{6,0},{1,7},{3,5},{5,3},{7,1},{8,14},{10,12},{12... | collective-permute-start | bytes 2359304 | tf_op jit(solution)/shard_map/ppermute | solution.py:22
  485.3 47.1 %collective-permute-start.25 = (bf16[192,2048]{1,0:T(8,128)(2,1)}, bf16[192,2048]{1,0:T(8,128)(2,1)S(1)}, u32[]{:S(2)}, u32[]{:S(2)}) collective-permute-start(bf16[192,2048]{1,0:T(8,128)(2,1)} %get-tuple-element.73), channel_id=1, source_target_pairs={{0,4},{2,6},{4,0},{6,2},{1,5},{3,7},{5,1},{7,3},{8,12},{10,14},{12... | collective-permute-start | bytes 2359304 | tf_op jit(solution)/shard_map/ppermute | solution.py:22
  495.0 115.3 %collective-permute-start.45 = (bf16[4,256,256]{2,1,0:T(8,128)(2,1)S(1)}, bf16[4,256,256]{2,1,0:T(8,128)(2,1)S(1)}, u32[]{:S(2)}, u32[]{:S(2)}) collective-permute-start(bf16[4,256,256]{2,1,0:T(8,128)(2,1)S(1)} %dynamic-slice_bitcast_fusion.4), channel_id=1, source_target_pairs={{0,1},{1,0},{2,3},{3,2},{4,5},{5,4},{6,7},{7,6},{8,9},{9,8},{10,11... | collective-permute-start | bytes 1572872 | tf_op jit(solution)/shard_map/ppermute | solution.py:22
  527.9 84.9 %collective-permute-start.49 = (bf16[256,1024]{1,0:T(8,128)(2,1)S(1)}, bf16[256,1024]{1,0:T(8,128)(2,1)S(1)}, u32[]{:S(2)}, u32[]{:S(2)}) collective-permute-start(bf16[256,1024]{1,0:T(8,128)(2,1)S(1)} %get-tuple-element.85), channel_id=1, source_target_pairs={{0,24},{8,16},{16,8},{24,0},{1,25},{9,17},{17,9},{25,1},{2,26},{10... | collective-permute-start | bytes 1572872 | tf_op jit(solution)/shard_map/ppermute | solution.py:22
  530.6 84.3 %collective-permute-start.51 = (bf16[256,1024]{1,0:T(8,128)(2,1)S(1)}, bf16[256,1024]{1,0:T(8,128)(2,1)S(1)}, u32[]{:S(2)}, u32[]{:S(2)}) collective-permute-start(bf16[256,1024]{1,0:T(8,128)(2,1)S(1)} %get-tuple-element.86), channel_id=1, source_target_pairs={{0,16},{8,24},{16,0},{24,8},{1,17},{9,25},{17,1},{25,9},{2,18},{10... | collective-permute-start | bytes 1572872 | tf_op jit(solution)/shard_map/ppermute | solution.py:22
  530.7 84.2 %collective-permute-start.50 = (bf16[256,1024]{1,0:T(8,128)(2,1)S(1)}, bf16[256,1024]{1,0:T(8,128)(2,1)S(1)}, u32[]{:S(2)}, u32[]{:S(2)}) collective-permute-start(bf16[256,1024]{1,0:T(8,128)(2,1)S(1)} %get-tuple-element.87), channel_id=1, source_target_pairs={{0,8},{8,0},{16,24},{24,16},{1,9},{9,1},{17,25},{25,17},{2,10},{10... | collective-permute-start | bytes 1572872 | tf_op jit(solution)/shard_map/ppermute | solution.py:22
  532.3 76.8 %collective-permute-start.44 = (f32[34,128]{1,0:T(8,128)S(1)}, f32[34,128]{1,0:T(8,128)S(1)}, u32[]{:S(2)}, u32[]{:S(2)}) collective-permute-start(f32[34,128]{1,0:T(8,128)S(1)} %add.322), channel_id=1, source_target_pairs={{0,16},{8,24},{16,0},{24,8},{1,17},{9,25},{17,1},{25,9},{2,18},{10... | collective-permute-start | bytes 52232 | tf_op jit(solution)/shard_map/ppermute | solution.py:22
  (67 other events, 1174.5 us)
Sparse Core Ops, SparseCore 0:
  10.2 58.6 all-gather.3
  70.6 77.8 all-gather.5
  150.1 90.8 all-gather.7
  391.8 79.9 reduce-scatter.2
  473.9 136.5 reduce-scatter.4
where the time goes:
time: 649 us; the launch traced here: 637 us
  waiting for transfers between devices  319 us (49%)
  matrix products  86.5 us (13%)
  starting transfers between devices  84.1 us (13%)
  Pallas kernels  56.4 us (9%)
  other arithmetic  47 us (7%)
  local copies, waits for them, and re-layouts  29 us (4%)
  between operations  14.8 us (2%)
    ppermute x52, waiting for transfers between devices, swap(): return lax.ppermute(value, axis, pairs(lax.axis_size(axis), k))  307 us
    ppermute x52, starting transfers between devices, swap(): return lax.ppermute(value, axis, pairs(lax.axis_size(axis), k))  83.9 us
    dot_general x11, matrix products, mm_nt(): lax.dot_general(a, b, (((1,), (1,)), ((), ())), preferred_element_type=F32)  41.9 us
    dot_general x5, matrix products, mm(): lax.dot_general(a, b, (((1,), (0,)), ((), ())), preferred_element_type=F32)  30.4 us
    pallas_call x1, Pallas kernels, per_device(): pl.pallas_call(attn_grad_kernel, grid_spec=pltpu.PrefetchScalarGridSpec(n...  19.3 us
    pallas_call x1, Pallas kernels, per_device(): pl.pallas_call(attn_kernel, grid_spec=pltpu.PrefetchScalarGridSpec(num_sc...  17.6 us
    dot_general x3, matrix products, mm_tn(): lax.dot_general(a, b, (((0,), (0,)), ((), ())), preferred_element_type=F32)  14.3 us
    pallas_call x1, Pallas kernels, expert_grads(): pl.pallas_call(expert_grad_kernel, grid=(width // tile,), in_specs=[pl.Bl...  13.9 us
  transfers between devices with their start and end apart: 57, of which 28 were waited for; matrix products, arithmetic and copies ran while one was open for 18% of the time, Pallas kernels for 6%

commit v1 on v0

--- a/solution.py
+++ b/solution.py
@@ -32,6 +32,23 @@
     for k in order_of(count):
         got[k] = swap(value, axis, k)
     return [got[k] for k in range(count)]
+
+
+def collect_crossed(value, axis):
+    if lax.axis_size(axis) != 4:
+        return jnp.concatenate(collect(value, axis), 0)
+    half = value.shape[1] // 2
+    low, high = value[:, :half], value[:, half:]
+
+    def send(part, k):
+        return swap(part, axis, k)
+
+    low_1, high_2 = send(low, 1), send(high, 2)
+    high_1, low_2 = send(high, 1), send(low, 2)
+    low_3, high_3 = swap(low_1, axis, 2), swap(high_2, axis, 1)
+    lows = jnp.concatenate([low, low_1, low_2, low_3], 0)
+    highs = jnp.concatenate([high, high_1, high_2, high_3], 0)
+    return jnp.concatenate([lows, highs], 1)
 
 
 def folded_positions(rows, count_ctx, half_block):
@@ -384,7 +401,7 @@
     kv_all = jnp.stack(collect(kv_own, "ctx"), 0).reshape(
         count_c, 2, count_s, seqs, own, head_dim
     )
-    full_query = full_qkv[:, :q_width]
+    full_query = lax.optimization_barrier(full_qkv[:, :q_width])
     queries = mm(normed_one, full_query).reshape(count_s, seqs, own, q_width)
     kv_weights = jnp.concatenate(collect(full_qkv[:, q_width:], "shard"), 1)
 
@@ -426,21 +443,42 @@
         ),
     )(me_ids, queries, kv_all, gain_q_row, cos_nat, sin_nat)
 
-    def reduce_blocks(block_of):
-        got = {}
-        for k in order_of(count_s):
-            got[k] = swap(block_of(k).astype(BF), "shard", k)
-        total = block_of(0).astype(F32)
-        for k in range(1, count_s):
-            total = total + got[k].astype(F32)
-        return total
-
-    attended = reduce_blocks(lambda k: mm_nt(attn[k].reshape(own_rows, q_width), full_out))
+    half_width = width // 2
+    sides = (slice(0, half_width), slice(half_width, width))
+
+    def reduce_blocks(term, crossed):
+        def send(value, k):
+            return swap(value.astype(BF), "shard", k)
+
+        low, high = sides
+        if count_s != 4 or not crossed:
+            full = slice(0, width)
+            got = {k: send(term(k, full), k) for k in order_of(count_s)}
+            total = term(0, full).astype(F32)
+            for part in got.values():
+                total = total + part.astype(F32)
+            return total
+        far_low = send(term(3, low), 1)
+        far_high = send(term(3, high), 2)
+        near_low = send(term(1, low), 1)
+        near_high = send(term(2, high), 2)
+        relay_low = swap((term(2, low).astype(F32) + far_low.astype(F32)).astype(BF), "shard", 2)
+        relay_high = swap((term(1, high).astype(F32) + far_high.astype(F32)).astype(BF), "shard", 1)
+        total_low = term(0, low).astype(F32) + near_low.astype(F32) + relay_low.astype(F32)
+        total_high = term(0, high).astype(F32) + near_high.astype(F32) + relay_high.astype(F32)
+        return jnp.concatenate([total_low, total_high], 1)
+
+    def block_rows_of(value):
+        return lambda k, columns: value[k * own_rows : (k + 1) * own_rows, columns]
+
+    attended = reduce_blocks(
+        lambda k, columns: mm_nt(attn[k].reshape(own_rows, q_width), full_out[columns]), True
+    )
     hidden = residual_own + attended
     inverse_two = inv_rms(hidden)
     hat_two = hidden * inverse_two
     normed_two = (hat_two * gain_mlp).astype(BF)
-    arrived = jnp.concatenate(collect(normed_two, "shard"), 0)
+    arrived = collect_crossed(normed_two, "shard")
 
     full_gate_up = full_experts[:, : 2 * hidden_width]
     full_down = full_experts[:, 2 * hidden_width :]
@@ -454,7 +492,7 @@
     grad_up = grad_inner * gate_act
     grad_gate_up = jnp.concatenate([grad_gate.astype(BF), grad_up.astype(BF)], 1)
     grad_slots = mm_nt(grad_gate_up, full_gate_up)
-    grad_normed_two = reduce_blocks(lambda k: grad_slots[k * own_rows : (k + 1) * own_rows])
+    grad_normed_two = reduce_blocks(block_rows_of(grad_slots.astype(BF)), True)
     grad_w_experts = expert_grads(arrived, grad_rows, after(grad_gate_up, grad_slots), inner_bf)
     sum_experts = scatter(grad_w_experts).astype(F32)
 
@@ -467,9 +505,9 @@
     weighted = weighted.astype(BF)
     route_part = jnp.sum(grad_all.astype(F32) * expert_out, -1)
     grad_hidden_bf = after(grad_hidden.astype(BF), grad_w_experts)
-    grad_att = jnp.concatenate(collect(grad_hidden_bf, "shard"), 0)
-    grad_att, weighted, route_part = lax.optimization_barrier((grad_att, weighted, route_part))
-    mixture = reduce_blocks(lambda k: weighted[k * own_rows : (k + 1) * own_rows])
+    grad_att = collect_crossed(grad_hidden_bf, "shard")
+    grad_att, weighted = lax.optimization_barrier((grad_att, weighted))
+    mixture = reduce_blocks(block_rows_of(weighted), False)
     block_out = (hidden + mixture).astype(BF)
     route_all = {0: route_part[:own_rows]}
     for k in order_of(count_s):
@@ -519,7 +557,8 @@
     grad_w_query = mm_tn(normed_one, grad_q).astype(BF)
     sum_query = scatter(grad_w_query).astype(F32)
     query_part = reduce_blocks(
-        lambda k: mm_nt(grad_q[k * own_rows : (k + 1) * own_rows], full_query)
+        lambda k, columns: mm_nt(grad_q[k * own_rows : (k + 1) * own_rows], full_query[columns]),
+        False,
     )
     grad_w_out = mm_tn(after(grad_att, grad_kv), attn.reshape(all_rows, q_width)).astype(BF)
     half_sum_out = sum_cores(grad_w_out)
@@ -542,10 +581,11 @@
         for k in order_of(count_s)
     }
     kv_rows[0] = grad_kv_bf[:own_rows]
-    sum_kv = sum_ctx(sum_cores(mm_tn(normed_one, grad_kv_bf).astype(BF)))
-    grad_normed_one = query_part + mm_nt(
-        jnp.concatenate([kv_rows[k] for k in range(count_s)], 1), kv_weights
-    )
+    half_sum_kv = sum_cores(mm_tn(normed_one, grad_kv_bf).astype(BF))
+    sum_kv = sum_ctx(half_sum_kv)
+    kv_all_rows = jnp.concatenate([kv_rows[k] for k in range(count_s)], 1)
+    kv_all_rows = after(kv_all_rows, half_sum_kv)
+    grad_normed_one = query_part + mm_nt(kv_all_rows, kv_weights)
     gain_attn_part = jnp.sum(grad_normed_one * hat_own, 0)
     grad_tokens = grad_hidden + norm_backward_step(
         grad_normed_one, hat_own, inverse_own, gain_attn
@@ -558,6 +598,8 @@
         while step < lax.axis_size(axis):
             gains = gains + swap(gains, axis, step)
             step *= 2
+        if axis == "shard":
+            gains, sum_experts = lax.optimization_barrier((gains, sum_experts))
     gains = gains.reshape(-1)
 
     def own_shape(value):

time: 649 us -> 590 us (0.909)
  waiting for transfers between devices: 319 us -> 192 us
  starting transfers between devices: 84.1 us -> 124 us
  other arithmetic: 47 us -> 75.7 us
    ppermute x52 -> x64, waiting for transfers between devices: 307 us -> 181 us  [swap(): return lax.ppermute(value, axis, pairs(lax.axis_size(axis), k))]
    ppermute x52 -> x64, starting transfers between devices: 83.9 us -> 124 us  [swap(): return lax.ppermute(value, axis, pairs(lax.axis_size(axis), k))]
    concatenate x2 -> x3, other arithmetic: 2.07 us -> 32.8 us  [the longest x2 31.9 us: collect_crossed(): return jnp.concatenate([lows, highs], 1)]
    dot_general x11 -> x15, matrix products: 41.9 us -> 38.7 us  [mm_nt(): lax.dot_general(a, b, (((1,), (1,)), ((), ())), preferred_element_type=F32)]
  transfers between devices with their start and end apart: 57 -> 69, of which waited for: 28 -> 31; matrix products, arithmetic and copies ran while one was open for 18% -> 28% of each run, Pallas kernels for 6% -> 7%
where the time goes in v1:
time: 590 us; the launch traced here: 581 us
  waiting for transfers between devices  192 us (33%)
  starting transfers between devices  124 us (21%)
  matrix products  82.4 us (14%)
  other arithmetic  75.7 us (13%)
  Pallas kernels  56.6 us (10%)
  local copies, waits for them, and re-layouts  34.9 us (6%)
  between operations  15 us (3%)
    ppermute x64, waiting for transfers between devices, swap(): return lax.ppermute(value, axis, pairs(lax.axis_size(axis), k))  181 us
    ppermute x64, starting transfers between devices, swap(): return lax.ppermute(value, axis, pairs(lax.axis_size(axis), k))  124 us
    dot_general x15, matrix products, mm_nt(): lax.dot_general(a, b, (((1,), (1,)), ((), ())), preferred_element_type=F32)  38.7 us
    concatenate x2, other arithmetic, collect_crossed(): return jnp.concatenate([lows, highs], 1)  31.9 us
    dot_general x5, matrix products, mm(): lax.dot_general(a, b, (((1,), (0,)), ((), ())), preferred_element_type=F32)  26.7 us
    pallas_call x1, Pallas kernels, per_device(): pl.pallas_call(attn_grad_kernel, grid_spec=pltpu.PrefetchScalarGridSpec(n...  19.5 us
    pallas_call x1, Pallas kernels, per_device(): pl.pallas_call(attn_kernel, grid_spec=pltpu.PrefetchScalarGridSpec(num_sc...  17.5 us
    dot_general x3, matrix products, mm_tn(): lax.dot_general(a, b, (((0,), (0,)), ((), ())), preferred_element_type=F32)  17.1 us
  transfers between devices with their start and end apart: 69, of which 31 were waited for; matrix products, arithmetic and copies ran while one was open for 28% of the time, Pallas kernels for 7%

profile of v1, /device:TPU:0, one launch (start us, length us, event | category | flops | bytes accessed | tf_op | source)
XLA Modules:
  0.0 580.8 jit_solution(2639538408038675051)
XLA Ops:
  24.8 6.3 %fusion.2 = bf16[768,2048]{1,0:T(8,128)(2,1)} fusion(f32[2048]{0:T(1024)S(1)} %copy-done.32, f32[768]{0:T(1024)S(1)} %add_rsqrt_fusion, bf16[192,2048]{1,0:T(8,128)(2,1)S(1)} %bitcast.146, bf16[192,2048]{1,0:T(8,128)(2,1)S(1)} %bitcast.148, bf16[192,2048]{1,0:T(8,128)(2,1)S(1)} %bitcast.144, bf16[192,2048]{1,0:T(8,128)(2,1)S(1)} %bitcast.135), kind=kLoop, calls=%fused_computation.7 | loop fusion | flops 17301504 | bytes 6302720 | tf_op jit(solution)/shard_map/convert_element_type | solution.py:362
  31.3 19.7 %collective-permute-done.4 = f32[192]{0:T(256)S(1)} collective-permute-done((f32[192]{0:T(256)S(1)}, f32[192]{0:T(256)S(1)}, u32[]{:S(2)}, u32[]{:S(2)}) %collective-permute-start.4) | collective-permute-done | bytes 800 | tf_op jit(solution)/shard_map/ppermute | solution.py:22
  58.3 10.7 %all-gather.4.cloned.1.call-done = bf16[2048,1280]{1,0:T(8,128)(2,1)} async-done(((bf16[256,1280]{1,0:T(8,128)(2,1)}), bf16[2048,1280]{1,0:T(8,128)(2,1)}) %all-gather.4.cloned.1.call-update) | async-done | bytes 5242896 | tf_op jit(solution)/shard_map/all_gather | solution.py:329
  88.2 11.1 %collective-permute-done.11 = bf16[2,768,128]{2,1,0:T(8,128)(2,1)S(1)} collective-permute-done((bf16[2,768,128]{2,1,0:T(8,128)(2,1)}, bf16[2,768,128]{2,1,0:T(8,128)(2,1)S(1)}, u32[]{:S(2)}, u32[]{:S(2)}) %collective-permute-start.11) | collective-permute-done | bytes 393248 | tf_op jit(solution)/shard_map/ppermute | solution.py:22
  99.3 26.7 %collective-permute-start.9 = (bf16[2,768,128]{2,1,0:T(8,128)(2,1)S(1)}, bf16[2,768,128]{2,1,0:T(8,128)(2,1)S(1)}, u32[]{:S(2)}, u32[]{:S(2)}) collective-permute-start(bf16[2,768,128]{2,1,0:T(8,128)(2,1)S(1)} %copy-done.15), channel_id=1, source_target_pairs={{0,8},{8,0},{16,24},{24,16},{1,9},{9,1},{17,25},{25,17},{2,10},{10... | collective-permute-start | bytes 1179656 | tf_op jit(solution)/shard_map/ppermute | solution.py:22
  126.0 5.1 fusion.87
  131.2 14.9 %collective-permute-done.10 = bf16[2,768,128]{2,1,0:T(8,128)(2,1)S(1)} collective-permute-done((bf16[2,768,128]{2,1,0:T(8,128)(2,1)S(1)}, bf16[2,768,128]{2,1,0:T(8,128)(2,1)S(1)}, u32[]{:S(2)}, u32[]{:S(2)}) %collective-permute-start.10) | collective-permute-done | bytes 393248 | tf_op jit(solution)/shard_map/ppermute | solution.py:22
  146.1 5.2 collective-permute-done.9
  154.9 17.5 %attn_fwd.1 = (bf16[4,3,64,1024]{3,2,1,0:T(8,128)(2,1)}, f32[3,8,256]{2,1,0:T(8,128)}, bf16[3,256,1024]{2,1,0:T(8,128)(2,1)}) custom-call(s32[2]{0:T(128)} %pad_add_fusion.ids_ref, f32[4,3,64,1024]{3,2,1,0:T(8,128)} %bitcast.196, bf16[4,2,4,3,64,128]{5,4,3,2,1,0:T(8,128)(2,1)} %pad_maximum_fusion.4.kv_ref, f32[1,128]{1,0:T(1,128)} %bitcast.194, ...), custom_call_target="tpu_custom_call" | custom-call | flops 3221225472 | bytes 12582912 | tf_op jit(solution)/shard_map/attn_fwd/pallas_call | solution.py:422
  186.0 13.3 %collective-permute-done.16 = bf16[192,1024]{1,0:T(8,128)(2,1)S(1)} collective-permute-done((bf16[192,1024]{1,0:T(8,128)(2,1)S(1)}, bf16[192,1024]{1,0:T(8,128)(2,1)S(1)}, u32[]{:S(2)}, u32[]{:S(2)}) %collective-permute-start.16) | collective-permute-done | bytes 393248 | tf_op jit(solution)/shard_map/ppermute | solution.py:22
  204.1 5.7 collective-permute-done.17
  216.9 7.9 %collective-permute-done.18 = bf16[192,1024]{1,0:T(8,128)(2,1)S(1)} collective-permute-done((bf16[192,1024]{1,0:T(8,128)(2,1)S(1)}, bf16[192,1024]{1,0:T(8,128)(2,1)S(1)}, u32[]{:S(2)}, u32[]{:S(2)}) %collective-permute-start.18) | collective-permute-done | bytes 393248 | tf_op jit(solution)/shard_map/ppermute | solution.py:22
  228.0 7.0 %collective-permute-done.19 = bf16[192,1024]{1,0:T(8,128)(2,1)S(1)} collective-permute-done((bf16[192,1024]{1,0:T(8,128)(2,1)S(1)}, bf16[192,1024]{1,0:T(8,128)(2,1)S(1)}, u32[]{:S(2)}, u32[]{:S(2)}) %collective-permute-start.19) | collective-permute-done | bytes 393248 | tf_op jit(solution)/shard_map/ppermute | solution.py:22
  235.0 4.6 collective-permute-done.20
  241.1 21.4 %maximum_maximum_fusion.rows_ref = bf16[768,2048]{1,0:T(8,128)(2,1)} fusion(bf16[192,1024]{1,0:T(8,128)(2,1)S(1)} %collective-permute-done.23, bf16[192,1024]{1,0:T(8,128)(2,1)S(1)} %collective-permute-done.22, bf16[192,1024]{1,0:T(8,128)(2,1)S(1)} %collective-permute-done.21, bf16[192,1024]{1,0:T(8,128)(2,1)S(1)} %get-tuple-element.112, ...), kind=kLoop, calls=%fused_computation.23 | loop fusion | flops 25165824 | bytes 6291456 | tf_op jit(solution)/shard_map/concatenate | solution.py:51
  262.5 8.5 %fusion.8 = f32[768,1536]{1,0:T(8,128)S(1)} fusion(bf16[2048,2304]{1,0:T(8,128)(2,1)} %all-gather.8.cloned.1.call-done, bf16[192,1024]{1,0:T(8,128)(2,1)} %copy-done.26, bf16[192,1024]{1,0:T(8,128)(2,1)} %copy-done.22, bf16[192,1024]{1,0:T(8,128)(2,1)} %copy-done.24, bf16[192,1024]{1,0:T(8,128)(2,1)S(1)} %get-tuple-element.112, ...), kind=kOutput, calls=%fused_computation.13 | convolution fusion | flops 4857004032 | bytes 14155776 | tf_op jit(solution)/shard_map/dot_general | solution.py:80
  277.1 6.5 %fusion.6 = bf16[768,2048]{1,0:T(8,128)(2,1)} fusion(bf16[2048,2304]{1,0:T(8,128)(2,1)S(1)} %copy-done.49, bf16[768,768]{1,0:T(8,128)(2,1)S(1)} %get-tuple-element.72, bf16[768,768]{1,0:T(8,128)(2,1)S(1)} %get-tuple-element.71), kind=kOutput, calls=%fused_computation.11 | convolution fusion | flops 4836556800 | bytes 11796480 | tf_op jit(solution)/shard_map/dot_general | solution.py:84
  283.6 13.9 %expert_grads.1 = bf16[2048,2304]{1,0:T(8,128)(2,1)} custom-call(bf16[768,2048]{1,0:T(8,128)(2,1)} %maximum_maximum_fusion.rows_ref, bf16[768,2048]{1,0:T(8,128)(2,1)} %fusion.3.grad_in_ref, bf16[768,1536]{1,0:T(8,128)(2,1)} %pad_maximum_fusion.3.grads_ref, bf16[768,768]{1,0:T(8,128)(2,1)} %get-tuple-element.73.inner_ref), custom_call_target="tpu_custom_call" | custom-call | flops 7247757312 | bytes 25165824 | tf_op jit(solution)/shard_map/expert_grads/pallas_call | solution.py:273
  302.7 8.1 %collective-permute-done.25 = bf16[192,1024]{1,0:T(8,128)(2,1)S(1)} collective-permute-done((bf16[192,1024]{1,0:T(8,128)(2,1)S(1)}, bf16[192,1024]{1,0:T(8,128)(2,1)S(1)}, u32[]{:S(2)}, u32[]{:S(2)}) %collective-permute-start.25) | collective-permute-done | bytes 393248 | tf_op jit(solution)/shard_map/ppermute | solution.py:22
  315.0 6.6 %collective-permute-done.26 = bf16[192,1024]{1,0:T(8,128)(2,1)S(1)} collective-permute-done((bf16[192,1024]{1,0:T(8,128)(2,1)S(1)}, bf16[192,1024]{1,0:T(8,128)(2,1)S(1)}, u32[]{:S(2)}, u32[]{:S(2)}) %collective-permute-start.26) | collective-permute-done | bytes 393248 | tf_op jit(solution)/shard_map/ppermute | solution.py:22
  340.2 6.5 %collective-permute-done.30 = bf16[192,1024]{1,0:T(8,128)(2,1)S(1)} collective-permute-done((bf16[192,1024]{1,0:T(8,128)(2,1)S(1)}, bf16[192,1024]{1,0:T(8,128)(2,1)S(1)}, u32[]{:S(2)}, u32[]{:S(2)}) %collective-permute-start.30) | collective-permute-done | bytes 393248 | tf_op jit(solution)/shard_map/ppermute | solution.py:22
  348.7 7.7 %fusion.5 = (f32[768]{0:T(1024)S(1)}, bf16[768,2048]{1,0:T(8,128)(2,1)}) fusion(bf16[192,2048]{1,0:T(8,128)(2,1)S(1)} %copy-done.19, bf16[192,2048]{1,0:T(8,128)(2,1)S(1)} %copy-done.21, bf16[192,2048]{1,0:T(8,128)(2,1)} %collective-permute-done.6, bf16[192,2048]{1,0:T(8,128)(2,1)S(1)} %bitcast.159, f32[768]{0:T(1024)S(1)} %copy-done.37, ...), kind=kOutput, calls=%fused_computation.10 | convolution fusion | flops 2437938432 | bytes 10622976 | tf_op jit(solution)/shard_map/dot_general | solution.py:84
  370.4 10.5 %maximum_maximum_fusion.1 = bf16[768,2048]{1,0:T(8,128)(2,1)S(1)} fusion(bf16[192,1024]{1,0:T(8,128)(2,1)} %collective-permute-done.35, bf16[192,1024]{1,0:T(8,128)(2,1)} %collective-permute-done.34, bf16[192,1024]{1,0:T(8,128)(2,1)} %collective-permute-done.33, bf16[192,1024]{1,0:T(8,128)(2,1)S(1)} %get-tuple-element.110, ...), kind=kLoop, calls=%fused_computation.24 | loop fusion | flops 25165824 | bytes 6291456 | tf_op jit(solution)/shard_map/concatenate | solution.py:51
  385.5 19.5 %attn_bwd.1 = (bf16[4,3,64,1024]{3,2,1,0:T(8,128)(2,1)}, bf16[4,2,4,3,64,128]{5,4,3,2,1,0:T(8,128)(2,1)}, f32[3,1,128]{2,1,0:T(1,128)}) custom-call(s32[2]{0:T(128)} %pad_add_fusion.ids_ref, bf16[3,256,1024]{2,1,0:T(8,128)(2,1)} %get-tuple-element.43.qb_ref, f32[4,3,64,1024]{3,2,1,0:T(8,128)} %bitcast.197, ...), custom_call_target="tpu_custom_call" | custom-call | flops 8053063680 | bytes 25165824 | tf_op jit(solution)/shard_map/attn_bwd/pallas_call | solution.py:521
  405.0 7.9 %convolution_convert_fusion = bf16[2048,1024]{1,0:T(8,128)(2,1)} fusion(bf16[768,2048]{1,0:T(8,128)(2,1)} %fusion.2, bf16[768,1024]{1,0:T(8,128)(2,1)} %bitcast.162), kind=kOutput, calls=%fused_computation.18 | convolution fusion | flops 3223322624 | bytes 8912896 | tf_op jit(solution)/shard_map/dot_general | solution.py:88
  414.2 5.8 %convolution_convert_fusion.1 = bf16[2048,1024]{1,0:T(8,128)(2,1)S(1)} fusion(bf16[768,2048]{1,0:T(8,128)(2,1)} %copy-done.6, bf16[768,1024]{1,0:T(8,128)(2,1)} %bitcast.161), kind=kOutput, calls=%fused_computation.19 | convolution fusion | flops 3223322624 | bytes 8912896 | tf_op jit(solution)/shard_map/dot_general | solution.py:88
  441.2 25.4 %collective-permute-done.43.refs_2_ = bf16[2,768,128]{2,1,0:T(8,128)(2,1)S(1)} collective-permute-done((bf16[2,768,128]{2,1,0:T(8,128)(2,1)S(1)}, bf16[2,768,128]{2,1,0:T(8,128)(2,1)S(1)}, u32[]{:S(2)}, u32[]{:S(2)}) %collective-permute-start.43) | collective-permute-done | bytes 393248 | tf_op jit(solution)/shard_map/ppermute | solution.py:22
  485.0 8.1 %collective-permute-done.47 = bf16[192,256]{1,0:T(8,128)(2,1)} collective-permute-done((bf16[192,256]{1,0:T(8,128)(2,1)}, bf16[192,256]{1,0:T(8,128)(2,1)}, u32[]{:S(2)}, u32[]{:S(2)}) %collective-permute-start.47) | collective-permute-done | bytes 98336 | tf_op jit(solution)/shard_map/ppermute | solution.py:22
  511.9 9.5 %collective-permute-start.63 = (bf16[256,1024]{1,0:T(8,128)(2,1)S(1)}, bf16[256,1024]{1,0:T(8,128)(2,1)S(1)}, u32[]{:S(2)}, u32[]{:S(2)}) collective-permute-start(bf16[256,1024]{1,0:T(8,128)(2,1)S(1)} %get-tuple-element.93), channel_id=1, source_target_pairs={{0,16},{8,24},{16,0},{24,8},{1,17},{9,25},{17,1},{25,9},{2,18},{10... | collective-permute-start | bytes 1572872 | tf_op jit(solution)/shard_map/ppermute | solution.py:22
  521.4 8.8 %collective-permute-start.62 = (bf16[256,1024]{1,0:T(8,128)(2,1)S(1)}, bf16[256,1024]{1,0:T(8,128)(2,1)S(1)}, u32[]{:S(2)}, u32[]{:S(2)}) collective-permute-start(bf16[256,1024]{1,0:T(8,128)(2,1)S(1)} %get-tuple-element.94), channel_id=1, source_target_pairs={{0,8},{8,0},{16,24},{24,16},{1,9},{9,1},{17,25},{25,17},{2,10},{10... | collective-permute-start | bytes 1572872 | tf_op jit(solution)/shard_map/ppermute | solution.py:22
  542.1 8.7 %collective-permute-start.60 = (bf16[256,256]{1,0:T(8,128)(2,1)S(1)}, bf16[256,256]{1,0:T(8,128)(2,1)S(1)}, u32[]{:S(2)}, u32[]{:S(2)}) collective-permute-start(bf16[256,256]{1,0:T(8,128)(2,1)S(1)} %get-tuple-element.114), channel_id=1, source_target_pairs={{0,16},{8,24},{16,0},{24,8},{1,17},{9,25},{17,1},{25,9},{2,18},{10... | collective-permute-start | bytes 393224 | tf_op jit(solution)/shard_map/ppermute | solution.py:22
  550.8 6.3 %collective-permute-done.63 = bf16[256,1024]{1,0:T(8,128)(2,1)S(1)} collective-permute-done((bf16[256,1024]{1,0:T(8,128)(2,1)S(1)}, bf16[256,1024]{1,0:T(8,128)(2,1)S(1)}, u32[]{:S(2)}, u32[]{:S(2)}) %collective-permute-start.63) | collective-permute-done | bytes 524320 | tf_op jit(solution)/shard_map/ppermute | solution.py:22
  (329 shorter events, 220.4 us)
Async XLA Ops:
  7.2 61.8 %all-gather.4.cloned.1.call-start = ((), (), s32[]{:S(2)}) async-start(), calls=%async_computation.2 | async-start | bytes 5898240 | tf_op jit(solution)/shard_map/all_gather | solution.py:329
  9.3 164.7 %all-gather.6.cloned.1.call-start = ((), (), s32[]{:S(2)}) async-start(), calls=%async_computation.3 | async-start | bytes 4718592 | tf_op jit(solution)/shard_map/all_gather | solution.py:329
  10.1 252.4 %all-gather.8.cloned.1.call-start = ((), (), s32[]{:S(2)}) async-start(), calls=%async_computation.4 | async-start | bytes 10616832 | tf_op jit(solution)/shard_map/all_gather | solution.py:329
  12.5 550.2 %reduce-scatter.3.cloned.1.call-start = ((), (), s32[]{:S(2)}) async-start(), calls=%async_computation.5 | async-start | bytes 10616832 | tf_op jit(solution)/shard_map/reduce_scatter | solution.py:332
  12.6 42.1 %collective-permute-start.8 = (bf16[192,2048]{1,0:T(8,128)(2,1)S(1)}, bf16[192,2048]{1,0:T(8,128)(2,1)S(1)}, u32[]{:S(2)}, u32[]{:S(2)}) collective-permute-start(bf16[192,2048]{1,0:T(8,128)(2,1)S(1)} %bitcast.155), channel_id=1, source_target_pairs={{0,6},{2,4},{4,2},{6,0},{1,7},{3,5},{5,3},{7,1},{8,14},{10,12},{12... | collective-permute-start | bytes 2359304 | tf_op jit(solution)/shard_map/ppermute | solution.py:22
  16.6 38.1 %collective-permute-start.7 = (bf16[192,2048]{1,0:T(8,128)(2,1)S(1)}, bf16[192,2048]{1,0:T(8,128)(2,1)S(1)}, u32[]{:S(2)}, u32[]{:S(2)}) collective-permute-start(bf16[192,2048]{1,0:T(8,128)(2,1)S(1)} %bitcast.156), channel_id=1, source_target_pairs={{0,4},{2,6},{4,0},{6,2},{1,5},{3,7},{5,1},{7,3},{8,12},{10,14},{12... | collective-permute-start | bytes 2359304 | tf_op jit(solution)/shard_map/ppermute | solution.py:22
  17.1 37.6 %collective-permute-start.6 = (bf16[192,2048]{1,0:T(8,128)(2,1)S(1)}, bf16[192,2048]{1,0:T(8,128)(2,1)}, u32[]{:S(2)}, u32[]{:S(2)}) collective-permute-start(bf16[192,2048]{1,0:T(8,128)(2,1)S(1)} %bitcast.157), channel_id=1, source_target_pairs={{0,2},{2,0},{4,6},{6,4},{1,3},{3,1},{5,7},{7,5},{8,10},{10,8},{12,... | collective-permute-start | bytes 2359304 | tf_op jit(solution)/shard_map/ppermute | solution.py:22
  17.3 33.7 %collective-permute-start.4 = (f32[192]{0:T(256)S(1)}, f32[192]{0:T(256)S(1)}, u32[]{:S(2)}, u32[]{:S(2)}) collective-permute-start(f32[192]{0:T(256)S(1)} %reduce_sum.131), channel_id=1, source_target_pairs={{0,4},{2,6},{4,0},{6,2},{1,5},{3,7},{5,1},{7,3},{8,12},{10,14},{12... | collective-permute-start | bytes 2312 | tf_op jit(solution)/shard_map/ppermute | solution.py:22
  19.3 33.5 %collective-permute-start.5 = (f32[192]{0:T(256)S(1)}, f32[192]{0:T(256)S(1)}, u32[]{:S(2)}, u32[]{:S(2)}) collective-permute-start(f32[192]{0:T(256)S(1)} %reduce_sum.133), channel_id=1, source_target_pairs={{0,6},{2,4},{4,2},{6,0},{1,7},{3,5},{5,3},{7,1},{8,14},{10,12},{12... | collective-permute-start | bytes 2312 | tf_op jit(solution)/shard_map/ppermute | solution.py:22
  80.5 72.1 %collective-permute-start.2 = (bf16[2048,256]{1,0:T(8,128)(2,1)S(1)}, bf16[2048,256]{1,0:T(8,128)(2,1)S(1)}, u32[]{:S(2)}, u32[]{:S(2)}) collective-permute-start(bf16[2048,256]{1,0:T(8,128)(2,1)S(1)} %slice.265), channel_id=1, source_target_pairs={{0,6},{2,4},{4,2},{6,0},{1,7},{3,5},{5,3},{7,1},{8,14},{10,12},{12... | collective-permute-start | bytes 3145736 | tf_op jit(solution)/shard_map/ppermute | solution.py:22
  83.2 69.4 %collective-permute-start.1 = (bf16[2048,256]{1,0:T(8,128)(2,1)S(1)}, bf16[2048,256]{1,0:T(8,128)(2,1)S(1)}, u32[]{:S(2)}, u32[]{:S(2)}) collective-permute-start(bf16[2048,256]{1,0:T(8,128)(2,1)S(1)} %slice.265), channel_id=1, source_target_pairs={{0,4},{2,6},{4,0},{6,2},{1,5},{3,7},{5,1},{7,3},{8,12},{10,14},{12... | collective-permute-start | bytes 3145736 | tf_op jit(solution)/shard_map/ppermute | solution.py:22
  83.7 68.9 %collective-permute-start = (bf16[2048,256]{1,0:T(8,128)(2,1)S(1)}, bf16[2048,256]{1,0:T(8,128)(2,1)S(1)}, u32[]{:S(2)}, u32[]{:S(2)}) collective-permute-start(bf16[2048,256]{1,0:T(8,128)(2,1)S(1)} %slice.265), channel_id=1, source_target_pairs={{0,2},{2,0},{4,6},{6,4},{1,3},{3,1},{5,7},{7,5},{8,10},{10,8},{12,... | collective-permute-start | bytes 3145736 | tf_op jit(solution)/shard_map/ppermute | solution.py:22
  84.7 61.4 %collective-permute-start.10 = (bf16[2,768,128]{2,1,0:T(8,128)(2,1)S(1)}, bf16[2,768,128]{2,1,0:T(8,128)(2,1)S(1)}, u32[]{:S(2)}, u32[]{:S(2)}) collective-permute-start(bf16[2,768,128]{2,1,0:T(8,128)(2,1)S(1)} %copy-done.15), channel_id=1, source_target_pairs={{0,16},{8,24},{16,0},{24,8},{1,17},{9,25},{17,1},{25,9},{2,18},{10... | collective-permute-start | bytes 1179656 | tf_op jit(solution)/shard_map/ppermute | solution.py:22
  99.3 52.0 %collective-permute-start.9 = (bf16[2,768,128]{2,1,0:T(8,128)(2,1)S(1)}, bf16[2,768,128]{2,1,0:T(8,128)(2,1)S(1)}, u32[]{:S(2)}, u32[]{:S(2)}) collective-permute-start(bf16[2,768,128]{2,1,0:T(8,128)(2,1)S(1)} %copy-done.15), channel_id=1, source_target_pairs={{0,8},{8,0},{16,24},{24,16},{1,9},{9,1},{17,25},{25,17},{2,10},{10... | collective-permute-start | bytes 1179656 | tf_op jit(solution)/shard_map/ppermute | solution.py:22
  176.7 33.3 %collective-permute-start.12 = (bf16[192,1024]{1,0:T(8,128)(2,1)S(1)}, bf16[192,1024]{1,0:T(8,128)(2,1)S(1)}, u32[]{:S(2)}, u32[]{:S(2)}) collective-permute-start(bf16[192,1024]{1,0:T(8,128)(2,1)S(1)} %fusion.43), channel_id=1, source_target_pairs={{0,2},{2,0},{4,6},{6,4},{1,3},{3,1},{5,7},{7,5},{8,10},{10,8},{12,... | collective-permute-start | bytes 1179656 | tf_op jit(solution)/shard_map/ppermute | solution.py:22
  180.6 23.5 %collective-permute-start.15 = (bf16[192,1024]{1,0:T(8,128)(2,1)S(1)}, bf16[192,1024]{1,0:T(8,128)(2,1)S(1)}, u32[]{:S(2)}, u32[]{:S(2)}) collective-permute-start(bf16[192,1024]{1,0:T(8,128)(2,1)S(1)} %fusion.49), channel_id=1, source_target_pairs={{0,4},{2,6},{4,0},{6,2},{1,5},{3,7},{5,1},{7,3},{8,12},{10,14},{12... | collective-permute-start | bytes 1179656 | tf_op jit(solution)/shard_map/ppermute | solution.py:22
  297.4 267.5 %reduce-scatter.5.cloned.1.call-start = ((), (), s32[]{:S(2)}) async-start(), calls=%async_computation.6 | async-start | bytes 4718592 | tf_op jit(solution)/shard_map/reduce_scatter | solution.py:332
  338.2 32.2 %collective-permute-start.31 = (bf16[192,1024]{1,0:T(8,128)(2,1)S(1)}, bf16[192,1024]{1,0:T(8,128)(2,1)}, u32[]{:S(2)}, u32[]{:S(2)}) collective-permute-start(bf16[192,1024]{1,0:T(8,128)(2,1)S(1)} %get-tuple-element.109), channel_id=1, source_target_pairs={{0,4},{2,6},{4,0},{6,2},{1,5},{3,7},{5,1},{7,3},{8,12},{10,14},{12... | collective-permute-start | bytes 1179656 | tf_op jit(solution)/shard_map/ppermute | solution.py:22
  338.6 31.8 %collective-permute-start.33 = (bf16[192,1024]{1,0:T(8,128)(2,1)S(1)}, bf16[192,1024]{1,0:T(8,128)(2,1)}, u32[]{:S(2)}, u32[]{:S(2)}) collective-permute-start(bf16[192,1024]{1,0:T(8,128)(2,1)S(1)} %get-tuple-element.110), channel_id=1, source_target_pairs={{0,2},{2,0},{4,6},{6,4},{1,3},{3,1},{5,7},{7,5},{8,10},{10,8},{12,... | collective-permute-start | bytes 1179656 | tf_op jit(solution)/shard_map/ppermute | solution.py:22
  346.7 23.7 %collective-permute-start.32 = (bf16[192,1024]{1,0:T(8,128)(2,1)S(1)}, bf16[192,1024]{1,0:T(8,128)(2,1)}, u32[]{:S(2)}, u32[]{:S(2)}) collective-permute-start(bf16[192,1024]{1,0:T(8,128)(2,1)S(1)} %collective-permute-done.30), channel_id=1, source_target_pairs={{0,4},{2,6},{4,0},{6,2},{1,5},{3,7},{5,1},{7,3},{8,12},{10,14},{12... | collective-permute-start | bytes 1179656 | tf_op jit(solution)/shard_map/ppermute | solution.py:22
  422.4 44.2 %collective-permute-start.43 = (bf16[2,768,128]{2,1,0:T(8,128)(2,1)S(1)}, bf16[2,768,128]{2,1,0:T(8,128)(2,1)S(1)}, u32[]{:S(2)}, u32[]{:S(2)}) collective-permute-start(bf16[2,768,128]{2,1,0:T(8,128)(2,1)S(1)} %bitcast.180), channel_id=1, source_target_pairs={{0,16},{8,24},{16,0},{24,8},{1,17},{9,25},{17,1},{25,9},{2,18},{10... | collective-permute-start | bytes 1179656 | tf_op jit(solution)/shard_map/ppermute | solution.py:22
  424.8 43.1 %collective-permute-start.44 = (bf16[2,768,128]{2,1,0:T(8,128)(2,1)S(1)}, bf16[2,768,128]{2,1,0:T(8,128)(2,1)S(1)}, u32[]{:S(2)}, u32[]{:S(2)}) collective-permute-start(bf16[2,768,128]{2,1,0:T(8,128)(2,1)S(1)} %bitcast.176), channel_id=1, source_target_pairs={{0,24},{8,16},{16,8},{24,0},{1,25},{9,17},{17,9},{25,1},{2,26},{10... | collective-permute-start | bytes 1179656 | tf_op jit(solution)/shard_map/ppermute | solution.py:22
  426.7 41.2 %collective-permute-start.42 = (bf16[2,768,128]{2,1,0:T(8,128)(2,1)S(1)}, bf16[2,768,128]{2,1,0:T(8,128)(2,1)S(1)}, u32[]{:S(2)}, u32[]{:S(2)}) collective-permute-start(bf16[2,768,128]{2,1,0:T(8,128)(2,1)S(1)} %bitcast.175), channel_id=1, source_target_pairs={{0,8},{8,0},{16,24},{24,16},{1,9},{9,1},{17,25},{25,17},{2,10},{10... | collective-permute-start | bytes 1179656 | tf_op jit(solution)/shard_map/ppermute | solution.py:22
  436.2 66.6 %collective-permute-start.40 = (bf16[192,2048]{1,0:T(8,128)(2,1)}, bf16[192,2048]{1,0:T(8,128)(2,1)}, u32[]{:S(2)}, u32[]{:S(2)}) collective-permute-start(bf16[192,2048]{1,0:T(8,128)(2,1)} %convolution_convert_fusion.5), channel_id=1, source_target_pairs={{0,2},{2,0},{4,6},{6,4},{1,3},{3,1},{5,7},{7,5},{8,10},{10,8},{12,... | collective-permute-start | bytes 2359304 | tf_op jit(solution)/shard_map/ppermute | solution.py:22
  437.6 66.2 %collective-permute-start.39 = (bf16[192,2048]{1,0:T(8,128)(2,1)}, bf16[192,2048]{1,0:T(8,128)(2,1)}, u32[]{:S(2)}, u32[]{:S(2)}) collective-permute-start(bf16[192,2048]{1,0:T(8,128)(2,1)} %convolution_convert_fusion.6), channel_id=1, source_target_pairs={{0,6},{2,4},{4,2},{6,0},{1,7},{3,5},{5,3},{7,1},{8,14},{10,12},{12... | collective-permute-start | bytes 2359304 | tf_op jit(solution)/shard_map/ppermute | solution.py:22
  466.6 39.8 %collective-permute-start.41 = (bf16[192,2048]{1,0:T(8,128)(2,1)}, bf16[192,2048]{1,0:T(8,128)(2,1)}, u32[]{:S(2)}, u32[]{:S(2)}) collective-permute-start(bf16[192,2048]{1,0:T(8,128)(2,1)} %convolution_convert_fusion.4), channel_id=1, source_target_pairs={{0,4},{2,6},{4,0},{6,2},{1,5},{3,7},{5,1},{7,3},{8,12},{10,14},{12... | collective-permute-start | bytes 2359304 | tf_op jit(solution)/shard_map/ppermute | solution.py:22
  500.9 33.6 %collective-permute-start.38 = (bf16[192,2048]{1,0:T(8,128)(2,1)}, bf16[192,2048]{1,0:T(8,128)(2,1)S(1)}, u32[]{:S(2)}, u32[]{:S(2)}) collective-permute-start(bf16[192,2048]{1,0:T(8,128)(2,1)} %get-tuple-element.77), channel_id=1, source_target_pairs={{0,4},{2,6},{4,0},{6,2},{1,5},{3,7},{5,1},{7,3},{8,12},{10,14},{12... | collective-permute-start | bytes 2359304 | tf_op jit(solution)/shard_map/ppermute | solution.py:22
  502.7 34.4 %collective-permute-start.37 = (bf16[192,2048]{1,0:T(8,128)(2,1)}, bf16[192,2048]{1,0:T(8,128)(2,1)S(1)}, u32[]{:S(2)}, u32[]{:S(2)}) collective-permute-start(bf16[192,2048]{1,0:T(8,128)(2,1)} %get-tuple-element.78), channel_id=1, source_target_pairs={{0,2},{2,0},{4,6},{6,4},{1,3},{3,1},{5,7},{7,5},{8,10},{10,8},{12,... | collective-permute-start | bytes 2359304 | tf_op jit(solution)/shard_map/ppermute | solution.py:22
  503.8 47.0 %collective-permute-start.61 = (bf16[256,1024]{1,0:T(8,128)(2,1)S(1)}, bf16[256,1024]{1,0:T(8,128)(2,1)S(1)}, u32[]{:S(2)}, u32[]{:S(2)}) collective-permute-start(bf16[256,1024]{1,0:T(8,128)(2,1)S(1)} %get-tuple-element.92), channel_id=1, source_target_pairs={{0,24},{8,16},{16,8},{24,0},{1,25},{9,17},{17,9},{25,1},{2,26},{10... | collective-permute-start | bytes 1572872 | tf_op jit(solution)/shard_map/ppermute | solution.py:22
  511.9 45.2 %collective-permute-start.63 = (bf16[256,1024]{1,0:T(8,128)(2,1)S(1)}, bf16[256,1024]{1,0:T(8,128)(2,1)S(1)}, u32[]{:S(2)}, u32[]{:S(2)}) collective-permute-start(bf16[256,1024]{1,0:T(8,128)(2,1)S(1)} %get-tuple-element.93), channel_id=1, source_target_pairs={{0,16},{8,24},{16,0},{24,8},{1,17},{9,25},{17,1},{25,9},{2,18},{10... | collective-permute-start | bytes 1572872 | tf_op jit(solution)/shard_map/ppermute | solution.py:22
  521.4 36.8 %collective-permute-start.62 = (bf16[256,1024]{1,0:T(8,128)(2,1)S(1)}, bf16[256,1024]{1,0:T(8,128)(2,1)S(1)}, u32[]{:S(2)}, u32[]{:S(2)}) collective-permute-start(bf16[256,1024]{1,0:T(8,128)(2,1)S(1)} %get-tuple-element.94), channel_id=1, source_target_pairs={{0,8},{8,0},{16,24},{24,16},{1,9},{9,1},{17,25},{25,17},{2,10},{10... | collective-permute-start | bytes 1572872 | tf_op jit(solution)/shard_map/ppermute | solution.py:22
  534.5 26.4 %collective-permute-start.58 = (bf16[256,256]{1,0:T(8,128)(2,1)S(1)}, bf16[256,256]{1,0:T(8,128)(2,1)S(1)}, u32[]{:S(2)}, u32[]{:S(2)}) collective-permute-start(bf16[256,256]{1,0:T(8,128)(2,1)S(1)} %get-tuple-element.113), channel_id=1, source_target_pairs={{0,24},{8,16},{16,8},{24,0},{1,25},{9,17},{17,9},{25,1},{2,26},{10... | collective-permute-start | bytes 393224 | tf_op jit(solution)/shard_map/ppermute | solution.py:22
  (90 other events, 913.5 us)
Sparse Core Ops, SparseCore 0:
  10.2 58.6 all-gather.3
  70.6 77.9 all-gather.5
  150.2 90.7 all-gather.7
  297.6 100.3 reduce-scatter.2
  413.0 81.3 reduce-scatter.4

commit v2 on v1

--- a/solution.py
+++ b/solution.py
@@ -34,9 +34,30 @@
     return [got[k] for k in range(count)]
 
 
-def collect_crossed(value, axis):
+def join_kernel(*refs):
+    *parts, out_ref = refs
+    rows, half = parts[0].shape
+    for k in range(len(parts) // 2):
+        out_ref[k * rows : (k + 1) * rows, :half] = parts[2 * k][...]
+        out_ref[k * rows : (k + 1) * rows, half:] = parts[2 * k + 1][...]
+
+
+def join(parts):
+    rows, half = parts[0].shape
+    shape = (len(parts) // 2 * rows, 2 * half)
+    return pl.pallas_call(
+        join_kernel,
+        out_shape=jax.ShapeDtypeStruct(shape, parts[0].dtype),
+        name="join",
+        cost_estimate=pl.CostEstimate(
+            flops=0, bytes_accessed=4 * shape[0] * shape[1], transcendentals=0
+        ),
+    )(*parts)
+
+
+def collect_crossed(value, axis, *others):
     if lax.axis_size(axis) != 4:
-        return jnp.concatenate(collect(value, axis), 0)
+        return after(jnp.concatenate(collect(value, axis), 0), *others)
     half = value.shape[1] // 2
     low, high = value[:, :half], value[:, half:]
 
@@ -46,9 +67,8 @@
     low_1, high_2 = send(low, 1), send(high, 2)
     high_1, low_2 = send(high, 1), send(low, 2)
     low_3, high_3 = swap(low_1, axis, 2), swap(high_2, axis, 1)
-    lows = jnp.concatenate([low, low_1, low_2, low_3], 0)
-    highs = jnp.concatenate([high, high_1, high_2, high_3], 0)
-    return jnp.concatenate([lows, highs], 1)
+    parts = (low, high, low_1, high_1, low_2, high_2, low_3, high_3)
+    return join(lax.optimization_barrier((*parts, *others))[: len(parts)])
 
 
 def folded_positions(rows, count_ctx, half_block):
@@ -341,11 +361,15 @@
             total = total + swap(sent, "dp", k).astype(F32)
         return total.astype(BF)
 
-    def sum_ctx(total):
+    def sum_ctx(total, *others):
         result = lax.dynamic_index_in_dim(total, me_c, 0, False).astype(F32)
+        parts = []
         for k in order_of(count_c):
             sent = lax.dynamic_index_in_dim(total, me_c ^ k, 0, False)
-            result = result + swap(sent, "ctx", k).astype(F32)
+            parts.append(swap(sent, "ctx", k))
+        parts = lax.optimization_barrier((*parts, *others))[: len(parts)]
+        for part in parts:
+            result = result + part.astype(F32)
         return result
 
     full_qkv = gather(jnp.concatenate([w_query, key_matrix, value_matrix], 1))
@@ -403,7 +427,10 @@
     )
     full_query = lax.optimization_barrier(full_qkv[:, :q_width])
     queries = mm(normed_one, full_query).reshape(count_s, seqs, own, q_width)
-    kv_weights = jnp.concatenate(collect(full_qkv[:, q_width:], "shard"), 1)
+    kv_weights = [full_qkv[:, q_width:]]
+    for k in range(1, count_s):
+        kv_weights.append(swap(kv_weights[0], "shard", k))
+    kv_weights = jnp.concatenate(kv_weights, 1)
 
     me_ids = jnp.stack([me_s, me_c]).astype(jnp.int32)
     row_spec = pl.BlockSpec((count_s, 1, own, q_width), lambda s, _: (0, s, 0, 0))
@@ -418,7 +445,6 @@
 
     table_spec = whole((block_rows, head_dim))
     gain_spec = whole((1, head_dim))
-    me_ids, kv_weights = lax.optimization_barrier((me_ids, kv_weights))
     attn, lse, queries_bf = pl.pallas_call(
         attn_kernel,
         grid_spec=pltpu.PrefetchScalarGridSpec(
@@ -478,7 +504,7 @@
     inverse_two = inv_rms(hidden)
     hat_two = hidden * inverse_two
     normed_two = (hat_two * gain_mlp).astype(BF)
-    arrived = collect_crossed(normed_two, "shard")
+    arrived = collect_crossed(normed_two, "shard", kv_weights)
 
     full_gate_up = full_experts[:, : 2 * hidden_width]
     full_down = full_experts[:, 2 * hidden_width :]
@@ -562,7 +588,6 @@
     )
     grad_w_out = mm_tn(after(grad_att, grad_kv), attn.reshape(all_rows, q_width)).astype(BF)
     half_sum_out = sum_cores(grad_w_out)
-    sum_out = sum_ctx(half_sum_out)
 
     kv_parts = [grad_kv[0]]
     for k in range(1, count_c):
@@ -582,9 +607,12 @@
     }
     kv_rows[0] = grad_kv_bf[:own_rows]
     half_sum_kv = sum_cores(mm_tn(normed_one, grad_kv_bf).astype(BF))
-    sum_kv = sum_ctx(half_sum_kv)
+    sum_kv = sum_ctx(half_sum_kv, sum_query)
     kv_all_rows = jnp.concatenate([kv_rows[k] for k in range(count_s)], 1)
-    kv_all_rows = after(kv_all_rows, half_sum_kv)
+    expert_parts = jnp.split(sum_experts[None], 3, 2)
+    kv_all_rows, _, *expert_parts = lax.optimization_barrier(
+        (kv_all_rows, half_sum_kv, *expert_parts)
+    )
     grad_normed_one = query_part + mm_nt(kv_all_rows, kv_weights)
     gain_attn_part = jnp.sum(grad_normed_one * hat_own, 0)
     grad_tokens = grad_hidden + norm_backward_step(
@@ -599,7 +627,7 @@
             gains = gains + swap(gains, axis, step)
             step *= 2
         if axis == "shard":
-            gains, sum_experts = lax.optimization_barrier((gains, sum_experts))
+            sum_out = sum_ctx(half_sum_out, gains)
     gains = gains.reshape(-1)
 
     def own_shape(value):
@@ -618,9 +646,7 @@
         sum_kv[:, :head_dim],
         sum_kv[:, head_dim:],
         sum_out,
-        sum_experts[None, :, :hidden_width],
-        sum_experts[None, :, hidden_width : 2 * hidden_width],
-        sum_experts[None, :, 2 * hidden_width :],
+        *expert_parts,
     )
 
 

time: 590 us -> 646 us (1.095)
  waiting for transfers between devices: 192 us -> 305 us
  other arithmetic: 75.7 us -> 46.3 us
  starting transfers between devices: 124 us -> 95.5 us
  local copies, waits for them, and re-layouts: 34.9 us -> 27.4 us
  Pallas kernels: 56.6 us -> 63.5 us
    reduce_scatter x2, waiting for transfers between devices: 0.02 us -> 81.3 us  [scatter(): return lax.psum_scatter(value, both, scatter_dimension=0, tiled=True)]
    concatenate x3 -> x0, other arithmetic: 34.1 us -> none  [the longest x2 31.9 us: collect_crossed(): return jnp.concatenate([lows, highs], 1)]
    ppermute x64, waiting for transfers between devices: 181 us -> 211 us  [swap(): return lax.ppermute(value, axis, pairs(lax.axis_size(axis), k))]
    ppermute x64, starting transfers between devices: 124 us -> 95.1 us  [swap(): return lax.ppermute(value, axis, pairs(lax.axis_size(axis), k))]
    pallas_call x0 -> x2, Pallas kernels: none -> 7.31 us  [join(): pl.pallas_call(join_kernel, out_shape=jax.ShapeDtypeStruct(shape, parts[0...]
  transfers between devices with their start and end apart: 69 -> 69, of which waited for: 31 -> 34; matrix products, arithmetic and copies ran while one was open for 28% -> 17% of each run, Pallas kernels for 7% -> 6%
where the time goes in v2:
time: 646 us; the launch traced here: 637 us
  waiting for transfers between devices  305 us (47%)
  starting transfers between devices  95.5 us (15%)
  matrix products  84.1 us (13%)
  Pallas kernels  63.5 us (10%)
  other arithmetic  46.3 us (7%)
  local copies, waits for them, and re-layouts  27.4 us (4%)
  between operations  15.1 us (2%)
    ppermute x64, waiting for transfers between devices, swap(): return lax.ppermute(value, axis, pairs(lax.axis_size(axis), k))  211 us
    ppermute x64, starting transfers between devices, swap(): return lax.ppermute(value, axis, pairs(lax.axis_size(axis), k))  95.1 us
    reduce_scatter x2, waiting for transfers between devices, scatter(): return lax.psum_scatter(value, both, scatter_dimension=0, tiled=True)  81.3 us
    dot_general x15, matrix products, mm_nt(): lax.dot_general(a, b, (((1,), (1,)), ((), ())), preferred_element_type=F32)  37.2 us
    dot_general x5, matrix products, mm(): lax.dot_general(a, b, (((1,), (0,)), ((), ())), preferred_element_type=F32)  30 us
    pallas_call x1, Pallas kernels, per_device(): pl.pallas_call(attn_grad_kernel, grid_spec=pltpu.PrefetchScalarGridSpec(n...  19.3 us
    pallas_call x1, Pallas kernels, per_device(): pl.pallas_call(attn_kernel, grid_spec=pltpu.PrefetchScalarGridSpec(num_sc...  17.4 us
    dot_general x3, matrix products, mm_tn(): lax.dot_general(a, b, (((0,), (0,)), ((), ())), preferred_element_type=F32)  16.9 us
  transfers between devices with their start and end apart: 69, of which 34 were waited for; matrix products, arithmetic and copies ran while one was open for 17% of the time, Pallas kernels for 6%

profile of v2, /device:TPU:0, one launch (start us, length us, event | category | flops | bytes accessed | tf_op | source)
XLA Modules:
  0.0 637.0 jit_solution(9790579053183842623)
XLA Ops:
  24.5 6.3 fusion.2
  31.6 18.3 %collective-permute-done.1 = f32[192]{0:T(256)S(1)} collective-permute-done((f32[192]{0:T(256)S(1)}, f32[192]{0:T(256)S(1)}, u32[]{:S(2)}, u32[]{:S(2)}) %collective-permute-start.1) | collective-permute-done | bytes 800 | tf_op jit(solution)/shard_map/ppermute | solution.py:22
  56.8 12.2 %all-gather.4.cloned.1.call-done = bf16[2048,1280]{1,0:T(8,128)(2,1)} async-done(((bf16[256,1280]{1,0:T(8,128)(2,1)}), bf16[2048,1280]{1,0:T(8,128)(2,1)}) %all-gather.4.cloned.1.call-update) | async-done | bytes 5242896 | tf_op jit(solution)/shard_map/all_gather | solution.py:349
  88.7 5.2 fusion.88
  93.8 5.4 collective-permute-done.8
  99.3 46.6 %collective-permute-done.7 = bf16[2,768,128]{2,1,0:T(8,128)(2,1)S(1)} collective-permute-done((bf16[2,768,128]{2,1,0:T(8,128)(2,1)}, bf16[2,768,128]{2,1,0:T(8,128)(2,1)S(1)}, u32[]{:S(2)}, u32[]{:S(2)}) %collective-permute-start.7) | collective-permute-done | bytes 393248 | tf_op jit(solution)/shard_map/ppermute | solution.py:22
  147.2 17.4 %attn_fwd.1 = (bf16[4,3,64,1024]{3,2,1,0:T(8,128)(2,1)}, f32[3,8,256]{2,1,0:T(8,128)}, bf16[3,256,1024]{2,1,0:T(8,128)(2,1)}) custom-call(s32[2]{0:T(128)} %pad_add_fusion.ids_ref, f32[4,3,64,1024]{3,2,1,0:T(8,128)} %bitcast.192, bf16[4,2,4,3,64,128]{5,4,3,2,1,0:T(8,128)(2,1)} %pad_maximum_fusion.4.kv_ref, f32[1,128]{1,0:T(1,128)} %bitcast.190, ...), custom_call_target="tpu_custom_call" | custom-call | flops 3221225472 | bytes 12582912 | tf_op jit(solution)/shard_map/attn_fwd/pallas_call | solution.py:448
  178.1 12.3 %collective-permute-done.13 = bf16[192,1024]{1,0:T(8,128)(2,1)S(1)} collective-permute-done((bf16[192,1024]{1,0:T(8,128)(2,1)S(1)}, bf16[192,1024]{1,0:T(8,128)(2,1)S(1)}, u32[]{:S(2)}, u32[]{:S(2)}) %collective-permute-start.13) | collective-permute-done | bytes 393248 | tf_op jit(solution)/shard_map/ppermute | solution.py:22
  195.8 4.5 collective-permute-done.14
  210.5 17.0 %collective-permute-done.22 = bf16[2048,256]{1,0:T(8,128)(2,1)} collective-permute-done((bf16[2048,256]{1,0:T(8,128)(2,1)}, bf16[2048,256]{1,0:T(8,128)(2,1)}, u32[]{:S(2)}, u32[]{:S(2)}) %collective-permute-start.22) | collective-permute-done | bytes 1048608 | tf_op jit(solution)/shard_map/ppermute | solution.py:22
  228.9 6.8 %collective-permute-done.18.refs_5_ = bf16[192,1024]{1,0:T(8,128)(2,1)S(1)} collective-permute-done((bf16[192,1024]{1,0:T(8,128)(2,1)S(1)}, bf16[192,1024]{1,0:T(8,128)(2,1)S(1)}, u32[]{:S(2)}, u32[]{:S(2)}) %collective-permute-start.18) | collective-permute-done | bytes 393248 | tf_op jit(solution)/shard_map/ppermute | solution.py:22
  238.7 4.6 collective-permute-done.16.refs_3_
  252.6 8.7 %fusion.8 = f32[768,1536]{1,0:T(8,128)S(1)} fusion(bf16[768,2048]{1,0:T(8,128)(2,1)} %join.2.rows_ref, bf16[2048,2304]{1,0:T(8,128)(2,1)} %all-gather.8.cloned.1.call-done), kind=kOutput, calls=%fused_computation.13 | convolution fusion | flops 4831838208 | bytes 14155776 | tf_op jit(solution)/shard_map/dot_general | solution.py:100
  261.3 4.4 multiply_convert_fusion.2
  265.7 5.3 fusion.6
  274.7 8.0 %collective-permute-done.25 = bf16[192,1024]{1,0:T(8,128)(2,1)S(1)} collective-permute-done((bf16[192,1024]{1,0:T(8,128)(2,1)S(1)}, bf16[192,1024]{1,0:T(8,128)(2,1)S(1)}, u32[]{:S(2)}, u32[]{:S(2)}) %collective-permute-start.25) | collective-permute-done | bytes 393248 | tf_op jit(solution)/shard_map/ppermute | solution.py:22
  287.0 6.7 %collective-permute-done.26 = bf16[192,1024]{1,0:T(8,128)(2,1)S(1)} collective-permute-done((bf16[192,1024]{1,0:T(8,128)(2,1)S(1)}, bf16[192,1024]{1,0:T(8,128)(2,1)S(1)}, u32[]{:S(2)}, u32[]{:S(2)}) %collective-permute-start.26) | collective-permute-done | bytes 393248 | tf_op jit(solution)/shard_map/ppermute | solution.py:22
  296.1 13.8 %expert_grads.1 = bf16[2048,2304]{1,0:T(8,128)(2,1)} custom-call(bf16[768,2048]{1,0:T(8,128)(2,1)} %join.2.rows_ref, bf16[768,2048]{1,0:T(8,128)(2,1)} %fusion.3.grad_in_ref, bf16[768,1536]{1,0:T(8,128)(2,1)} %pad_maximum_fusion.3.grads_ref, bf16[768,768]{1,0:T(8,128)(2,1)} %get-tuple-element.115.inner_ref), custom_call_target="tpu_custom_call" | custom-call | flops 7247757312 | bytes 25165824 | tf_op jit(solution)/shard_map/expert_grads/pallas_call | solution.py:293
  321.8 6.8 %collective-permute-done.33.refs_5_ = bf16[192,1024]{1,0:T(8,128)(2,1)S(1)} collective-permute-done((bf16[192,1024]{1,0:T(8,128)(2,1)S(1)}, bf16[192,1024]{1,0:T(8,128)(2,1)S(1)}, u32[]{:S(2)}, u32[]{:S(2)}) %collective-permute-start.33) | collective-permute-done | bytes 393248 | tf_op jit(solution)/shard_map/ppermute | solution.py:22
  330.8 7.4 %fusion.5 = (f32[768]{0:T(1024)S(1)}, bf16[768,2048]{1,0:T(8,128)(2,1)}) fusion(bf16[192,2048]{1,0:T(8,128)(2,1)} %collective-permute-done.5, bf16[192,2048]{1,0:T(8,128)(2,1)} %collective-permute-done.4, bf16[192,2048]{1,0:T(8,128)(2,1)} %collective-permute-done.3, bf16[192,2048]{1,0:T(8,128)(2,1)S(1)} %bitcast.156, f32[768]{0:T(1024)S(1)} %copy-done.44, ...), kind=kOutput, calls=%fused_computation.10 | convolution fusion | flops 2437938432 | bytes 10622976 | tf_op jit(solution)/shard_map/dot_general | solution.py:104
  343.6 7.7 %convolution_convert_fusion.7 = bf16[768,1024]{1,0:T(8,128)(2,1)} fusion(bf16[768,2048]{1,0:T(8,128)(2,1)} %join.3, bf16[2048,1024]{1,0:T(8,128)(2,1)} %all-gather.6.cloned.1.call-done), kind=kOutput, calls=%fused_computation.44 | convolution fusion | flops 3222011904 | bytes 8912896 | tf_op jit(solution)/shard_map/dot_general | solution.py:100
  351.3 19.3 %attn_bwd.1 = (bf16[4,3,64,1024]{3,2,1,0:T(8,128)(2,1)}, bf16[4,2,4,3,64,128]{5,4,3,2,1,0:T(8,128)(2,1)}, f32[3,1,128]{2,1,0:T(1,128)}) custom-call(s32[2]{0:T(128)} %pad_add_fusion.ids_ref, bf16[3,256,1024]{2,1,0:T(8,128)(2,1)} %get-tuple-element.79.qb_ref, f32[4,3,64,1024]{3,2,1,0:T(8,128)} %bitcast.193, ...), custom_call_target="tpu_custom_call" | custom-call | flops 8053063680 | bytes 25165824 | tf_op jit(solution)/shard_map/attn_bwd/pallas_call | solution.py:547
  370.6 7.9 %convolution_convert_fusion = bf16[2048,1024]{1,0:T(8,128)(2,1)} fusion(bf16[768,2048]{1,0:T(8,128)(2,1)} %fusion.2, bf16[768,1024]{1,0:T(8,128)(2,1)} %bitcast.159), kind=kOutput, calls=%fused_computation.18 | convolution fusion | flops 3223322624 | bytes 8912896 | tf_op jit(solution)/shard_map/dot_general | solution.py:108
  386.1 5.8 convolution_convert_fusion.1
  396.0 7.8 %collective-permute-start.44 = (bf16[2,768,128]{2,1,0:T(8,128)(2,1)S(1)}, bf16[2,768,128]{2,1,0:T(8,128)(2,1)}, u32[]{:S(2)}, u32[]{:S(2)}) collective-permute-start(bf16[2,768,128]{2,1,0:T(8,128)(2,1)S(1)} %bitcast.175), channel_id=1, source_target_pairs={{0,24},{8,16},{16,8},{24,0},{1,25},{9,17},{17,9},{25,1},{2,26},{10... | collective-permute-start | bytes 1179656 | tf_op jit(solution)/shard_map/ppermute | solution.py:22
  414.3 4.7 fusion.10
  419.0 22.6 %collective-permute-done.43.refs_2_ = bf16[2,768,128]{2,1,0:T(8,128)(2,1)} collective-permute-done((bf16[2,768,128]{2,1,0:T(8,128)(2,1)}, bf16[2,768,128]{2,1,0:T(8,128)(2,1)}, u32[]{:S(2)}, u32[]{:S(2)}) %collective-permute-start.43) | collective-permute-done | bytes 393248 | tf_op jit(solution)/shard_map/ppermute | solution.py:22
  456.5 16.5 %collective-permute-start.60 = (bf16[256,256]{1,0:T(8,128)(2,1)}, bf16[256,256]{1,0:T(8,128)(2,1)S(1)}, u32[]{:S(2)}, u32[]{:S(2)}) collective-permute-start(bf16[256,256]{1,0:T(8,128)(2,1)} %get-tuple-element.155), channel_id=1, source_target_pairs={{0,16},{8,24},{16,0},{24,8},{1,17},{9,25},{17,1},{25,9},{2,18},{10... | collective-permute-start | bytes 393224 | tf_op jit(solution)/shard_map/ppermute | solution.py:22
  492.1 81.3 %reduce-scatter.3.cloned.1.call-done = bf16[256,2304]{1,0:T(8,128)(2,1)} async-done(((bf16[2048,2304]{1,0:T(8,128)(2,1)}), bf16[256,2304]{1,0:T(8,128)(2,1)}) %reduce-scatter.3.cloned.1.call-update) | async-done | bytes 1179664 | tf_op jit(solution)/shard_map/reduce_scatter | solution.py:352
  587.0 7.3 %collective-permute-done.54 = f32[34,128]{1,0:T(8,128)S(1)} collective-permute-done((f32[34,128]{1,0:T(8,128)S(1)}, f32[34,128]{1,0:T(8,128)S(1)}, u32[]{:S(2)}, u32[]{:S(2)}) %collective-permute-start.54) | collective-permute-done | bytes 17440 | tf_op jit(solution)/shard_map/ppermute | solution.py:22
  602.4 4.3 fusion.21
  606.6 17.4 %collective-permute-done.62 = bf16[256,1024]{1,0:T(8,128)(2,1)S(1)} collective-permute-done((bf16[256,1024]{1,0:T(8,128)(2,1)S(1)}, bf16[256,1024]{1,0:T(8,128)(2,1)S(1)}, u32[]{:S(2)}, u32[]{:S(2)}) %collective-permute-start.62) | collective-permute-done | bytes 524320 | tf_op jit(solution)/shard_map/ppermute | solution.py:22
  (332 shorter events, 201.8 us)
Async XLA Ops:
  7.2 61.8 %all-gather.4.cloned.1.call-start = ((), (), s32[]{:S(2)}) async-start(), calls=%async_computation.2 | async-start | bytes 5898240 | tf_op jit(solution)/shard_map/all_gather | solution.py:349
  9.4 156.8 %all-gather.6.cloned.1.call-start = ((), (), s32[]{:S(2)}) async-start(), calls=%async_computation.3 | async-start | bytes 4718592 | tf_op jit(solution)/shard_map/all_gather | solution.py:349
  10.1 242.5 %all-gather.8.cloned.1.call-start = ((), (), s32[]{:S(2)}) async-start(), calls=%async_computation.4 | async-start | bytes 10616832 | tf_op jit(solution)/shard_map/all_gather | solution.py:349
  11.3 468.0 %reduce-scatter.5.cloned.1.call-start = ((), (), s32[]{:S(2)}) async-start(), calls=%async_computation.6 | async-start | bytes 4718592 | tf_op jit(solution)/shard_map/reduce_scatter | solution.py:352
  11.4 42.2 %collective-permute-start.5 = (bf16[192,2048]{1,0:T(8,128)(2,1)S(1)}, bf16[192,2048]{1,0:T(8,128)(2,1)}, u32[]{:S(2)}, u32[]{:S(2)}) collective-permute-start(bf16[192,2048]{1,0:T(8,128)(2,1)S(1)} %bitcast.152), channel_id=1, source_target_pairs={{0,6},{2,4},{4,2},{6,0},{1,7},{3,5},{5,3},{7,1},{8,14},{10,12},{12... | collective-permute-start | bytes 2359304 | tf_op jit(solution)/shard_map/ppermute | solution.py:22
  15.4 38.2 %collective-permute-start.4 = (bf16[192,2048]{1,0:T(8,128)(2,1)S(1)}, bf16[192,2048]{1,0:T(8,128)(2,1)}, u32[]{:S(2)}, u32[]{:S(2)}) collective-permute-start(bf16[192,2048]{1,0:T(8,128)(2,1)S(1)} %bitcast.153), channel_id=1, source_target_pairs={{0,4},{2,6},{4,0},{6,2},{1,5},{3,7},{5,1},{7,3},{8,12},{10,14},{12... | collective-permute-start | bytes 2359304 | tf_op jit(solution)/shard_map/ppermute | solution.py:22
  15.9 37.7 %collective-permute-start.3 = (bf16[192,2048]{1,0:T(8,128)(2,1)S(1)}, bf16[192,2048]{1,0:T(8,128)(2,1)}, u32[]{:S(2)}, u32[]{:S(2)}) collective-permute-start(bf16[192,2048]{1,0:T(8,128)(2,1)S(1)} %bitcast.154), channel_id=1, source_target_pairs={{0,2},{2,0},{4,6},{6,4},{1,3},{3,1},{5,7},{7,5},{8,10},{10,8},{12,... | collective-permute-start | bytes 2359304 | tf_op jit(solution)/shard_map/ppermute | solution.py:22
  16.1 33.8 %collective-permute-start.1 = (f32[192]{0:T(256)S(1)}, f32[192]{0:T(256)S(1)}, u32[]{:S(2)}, u32[]{:S(2)}) collective-permute-start(f32[192]{0:T(256)S(1)} %reduce_sum.131), channel_id=1, source_target_pairs={{0,4},{2,6},{4,0},{6,2},{1,5},{3,7},{5,1},{7,3},{8,12},{10,14},{12... | collective-permute-start | bytes 2312 | tf_op jit(solution)/shard_map/ppermute | solution.py:22
  18.1 34.1 %collective-permute-start.2 = (f32[192]{0:T(256)S(1)}, f32[192]{0:T(256)S(1)}, u32[]{:S(2)}, u32[]{:S(2)}) collective-permute-start(f32[192]{0:T(256)S(1)} %reduce_sum.133), channel_id=1, source_target_pairs={{0,6},{2,4},{4,2},{6,0},{1,7},{3,5},{5,3},{7,1},{8,14},{10,12},{12... | collective-permute-start | bytes 2312 | tf_op jit(solution)/shard_map/ppermute | solution.py:22
  77.8 68.0 %collective-permute-start.7 = (bf16[2,768,128]{2,1,0:T(8,128)(2,1)}, bf16[2,768,128]{2,1,0:T(8,128)(2,1)S(1)}, u32[]{:S(2)}, u32[]{:S(2)}) collective-permute-start(bf16[2,768,128]{2,1,0:T(8,128)(2,1)} %key_prep.1), channel_id=1, source_target_pairs={{0,16},{8,24},{16,0},{24,8},{1,17},{9,25},{17,1},{25,9},{2,18},{10... | collective-permute-start | bytes 1179656 | tf_op jit(solution)/shard_map/ppermute | solution.py:22
  78.3 67.6 %collective-permute-start.6 = (bf16[2,768,128]{2,1,0:T(8,128)(2,1)}, bf16[2,768,128]{2,1,0:T(8,128)(2,1)S(1)}, u32[]{:S(2)}, u32[]{:S(2)}) collective-permute-start(bf16[2,768,128]{2,1,0:T(8,128)(2,1)} %key_prep.1), channel_id=1, source_target_pairs={{0,8},{8,0},{16,24},{24,16},{1,9},{9,1},{17,25},{25,17},{2,10},{10... | collective-permute-start | bytes 1179656 | tf_op jit(solution)/shard_map/ppermute | solution.py:22
  83.7 126.2 %collective-permute-start.23 = (bf16[2048,256]{1,0:T(8,128)(2,1)}, bf16[2048,256]{1,0:T(8,128)(2,1)}, u32[]{:S(2)}, u32[]{:S(2)}) collective-permute-start(bf16[2048,256]{1,0:T(8,128)(2,1)} %slice.254), channel_id=1, source_target_pairs={{0,6},{2,4},{4,2},{6,0},{1,7},{3,5},{5,3},{7,1},{8,14},{10,12},{12... | collective-permute-start | bytes 3145736 | tf_op jit(solution)/shard_map/ppermute | solution.py:22
  168.8 32.3 %collective-permute-start.9 = (bf16[192,1024]{1,0:T(8,128)(2,1)S(1)}, bf16[192,1024]{1,0:T(8,128)(2,1)S(1)}, u32[]{:S(2)}, u32[]{:S(2)}) collective-permute-start(bf16[192,1024]{1,0:T(8,128)(2,1)S(1)} %fusion.43), channel_id=1, source_target_pairs={{0,2},{2,0},{4,6},{6,4},{1,3},{3,1},{5,7},{7,5},{8,10},{10,8},{12,... | collective-permute-start | bytes 1179656 | tf_op jit(solution)/shard_map/ppermute | solution.py:22
  195.2 32.2 %collective-permute-start.22 = (bf16[2048,256]{1,0:T(8,128)(2,1)}, bf16[2048,256]{1,0:T(8,128)(2,1)}, u32[]{:S(2)}, u32[]{:S(2)}) collective-permute-start(bf16[2048,256]{1,0:T(8,128)(2,1)} %slice.254), channel_id=1, source_target_pairs={{0,4},{2,6},{4,0},{6,2},{1,5},{3,7},{5,1},{7,3},{8,12},{10,14},{12... | collective-permute-start | bytes 3145736 | tf_op jit(solution)/shard_map/ppermute | solution.py:22
  200.3 38.4 %collective-permute-start.21 = (bf16[2048,256]{1,0:T(8,128)(2,1)}, bf16[2048,256]{1,0:T(8,128)(2,1)}, u32[]{:S(2)}, u32[]{:S(2)}) collective-permute-start(bf16[2048,256]{1,0:T(8,128)(2,1)} %slice.254), channel_id=1, source_target_pairs={{0,2},{2,0},{4,6},{6,4},{1,3},{3,1},{5,7},{7,5},{8,10},{10,8},{12,... | collective-permute-start | bytes 3145736 | tf_op jit(solution)/shard_map/ppermute | solution.py:22
  206.9 28.8 %collective-permute-start.18 = (bf16[192,1024]{1,0:T(8,128)(2,1)S(1)}, bf16[192,1024]{1,0:T(8,128)(2,1)S(1)}, u32[]{:S(2)}, u32[]{:S(2)}) collective-permute-start(bf16[192,1024]{1,0:T(8,128)(2,1)S(1)} %get-tuple-element.61.refs_1_), channel_id=1, source_target_pairs={{0,4},{2,6},{4,0},{6,2},{1,5},{3,7},{5,1},{7,3},{8,12},{10,14},{12... | collective-permute-start | bytes 1179656 | tf_op jit(solution)/shard_map/ppermute | solution.py:22
  208.5 28.8 %collective-permute-start.15 = (bf16[192,1024]{1,0:T(8,128)(2,1)S(1)}, bf16[192,1024]{1,0:T(8,128)(2,1)S(1)}, u32[]{:S(2)}, u32[]{:S(2)}) collective-permute-start(bf16[192,1024]{1,0:T(8,128)(2,1)S(1)} %get-tuple-element.60.refs_0_), channel_id=1, source_target_pairs={{0,2},{2,0},{4,6},{6,4},{1,3},{3,1},{5,7},{7,5},{8,10},{10,8},{12,... | collective-permute-start | bytes 1179656 | tf_op jit(solution)/shard_map/ppermute | solution.py:22
  209.9 33.4 %collective-permute-start.16 = (bf16[192,1024]{1,0:T(8,128)(2,1)S(1)}, bf16[192,1024]{1,0:T(8,128)(2,1)S(1)}, u32[]{:S(2)}, u32[]{:S(2)}) collective-permute-start(bf16[192,1024]{1,0:T(8,128)(2,1)S(1)} %get-tuple-element.61.refs_1_), channel_id=1, source_target_pairs={{0,2},{2,0},{4,6},{6,4},{1,3},{3,1},{5,7},{7,5},{8,10},{10,8},{12,... | collective-permute-start | bytes 1179656 | tf_op jit(solution)/shard_map/ppermute | solution.py:22
  286.1 23.8 %collective-permute-start.27 = (bf16[192,1024]{1,0:T(8,128)(2,1)S(1)}, bf16[192,1024]{1,0:T(8,128)(2,1)}, u32[]{:S(2)}, u32[]{:S(2)}) collective-permute-start(bf16[192,1024]{1,0:T(8,128)(2,1)S(1)} %get-tuple-element.124), channel_id=1, source_target_pairs={{0,4},{2,6},{4,0},{6,2},{1,5},{3,7},{5,1},{7,3},{8,12},{10,14},{12... | collective-permute-start | bytes 1179656 | tf_op jit(solution)/shard_map/ppermute | solution.py:22
  378.5 194.9 %reduce-scatter.3.cloned.1.call-start = ((), (), s32[]{:S(2)}) async-start(), calls=%async_computation.5 | async-start | bytes 10616832 | tf_op jit(solution)/shard_map/reduce_scatter | solution.py:352
  396.0 45.6 %collective-permute-start.43 = (bf16[2,768,128]{2,1,0:T(8,128)(2,1)}, bf16[2,768,128]{2,1,0:T(8,128)(2,1)}, u32[]{:S(2)}, u32[]{:S(2)}) collective-permute-start(bf16[2,768,128]{2,1,0:T(8,128)(2,1)} %bitcast.35), channel_id=1, source_target_pairs={{0,16},{8,24},{16,0},{24,8},{1,17},{9,25},{17,1},{25,9},{2,18},{10... | collective-permute-start | bytes 1179656 | tf_op jit(solution)/shard_map/ppermute | solution.py:22
  396.0 45.6 %collective-permute-start.44 = (bf16[2,768,128]{2,1,0:T(8,128)(2,1)S(1)}, bf16[2,768,128]{2,1,0:T(8,128)(2,1)}, u32[]{:S(2)}, u32[]{:S(2)}) collective-permute-start(bf16[2,768,128]{2,1,0:T(8,128)(2,1)S(1)} %bitcast.175), channel_id=1, source_target_pairs={{0,24},{8,16},{16,8},{24,0},{1,25},{9,17},{17,9},{25,1},{2,26},{10... | collective-permute-start | bytes 1179656 | tf_op jit(solution)/shard_map/ppermute | solution.py:22
  403.8 39.0 %collective-permute-start.42 = (bf16[2,768,128]{2,1,0:T(8,128)(2,1)S(1)}, bf16[2,768,128]{2,1,0:T(8,128)(2,1)}, u32[]{:S(2)}, u32[]{:S(2)}) collective-permute-start(bf16[2,768,128]{2,1,0:T(8,128)(2,1)S(1)} %bitcast.172), channel_id=1, source_target_pairs={{0,8},{8,0},{16,24},{24,16},{1,9},{9,1},{17,25},{25,17},{2,10},{10... | collective-permute-start | bytes 1179656 | tf_op jit(solution)/shard_map/ppermute | solution.py:22
  456.5 27.2 %collective-permute-start.60 = (bf16[256,256]{1,0:T(8,128)(2,1)}, bf16[256,256]{1,0:T(8,128)(2,1)S(1)}, u32[]{:S(2)}, u32[]{:S(2)}) collective-permute-start(bf16[256,256]{1,0:T(8,128)(2,1)} %get-tuple-element.155), channel_id=1, source_target_pairs={{0,16},{8,24},{16,0},{24,8},{1,17},{9,25},{17,1},{25,9},{2,18},{10... | collective-permute-start | bytes 393224 | tf_op jit(solution)/shard_map/ppermute | solution.py:22
  475.8 100.6 %collective-permute-start.40 = (bf16[192,2048]{1,0:T(8,128)(2,1)}, bf16[192,2048]{1,0:T(8,128)(2,1)}, u32[]{:S(2)}, u32[]{:S(2)}) collective-permute-start(bf16[192,2048]{1,0:T(8,128)(2,1)} %convolution_convert_fusion.5), channel_id=1, source_target_pairs={{0,2},{2,0},{4,6},{6,4},{1,3},{3,1},{5,7},{7,5},{8,10},{10,8},{12,... | collective-permute-start | bytes 2359304 | tf_op jit(solution)/shard_map/ppermute | solution.py:22
  477.0 100.5 %collective-permute-start.39 = (bf16[192,2048]{1,0:T(8,128)(2,1)}, bf16[192,2048]{1,0:T(8,128)(2,1)}, u32[]{:S(2)}, u32[]{:S(2)}) collective-permute-start(bf16[192,2048]{1,0:T(8,128)(2,1)} %convolution_convert_fusion.6), channel_id=1, source_target_pairs={{0,6},{2,4},{4,2},{6,0},{1,7},{3,5},{5,3},{7,1},{8,14},{10,12},{12... | collective-permute-start | bytes 2359304 | tf_op jit(solution)/shard_map/ppermute | solution.py:22
  483.8 96.0 %collective-permute-start.41 = (bf16[192,2048]{1,0:T(8,128)(2,1)}, bf16[192,2048]{1,0:T(8,128)(2,1)}, u32[]{:S(2)}, u32[]{:S(2)}) collective-permute-start(bf16[192,2048]{1,0:T(8,128)(2,1)} %convolution_convert_fusion.4), channel_id=1, source_target_pairs={{0,4},{2,6},{4,0},{6,2},{1,5},{3,7},{5,1},{7,3},{8,12},{10,14},{12... | collective-permute-start | bytes 2359304 | tf_op jit(solution)/shard_map/ppermute | solution.py:22
  485.5 115.5 %collective-permute-start.36 = (bf16[192,2048]{1,0:T(8,128)(2,1)}, bf16[192,2048]{1,0:T(8,128)(2,1)}, u32[]{:S(2)}, u32[]{:S(2)}) collective-permute-start(bf16[192,2048]{1,0:T(8,128)(2,1)} %get-tuple-element.118), channel_id=1, source_target_pairs={{0,6},{2,4},{4,2},{6,0},{1,7},{3,5},{5,3},{7,1},{8,14},{10,12},{12... | collective-permute-start | bytes 2359304 | tf_op jit(solution)/shard_map/ppermute | solution.py:22
  491.1 111.2 %collective-permute-start.38 = (bf16[192,2048]{1,0:T(8,128)(2,1)}, bf16[192,2048]{1,0:T(8,128)(2,1)}, u32[]{:S(2)}, u32[]{:S(2)}) collective-permute-start(bf16[192,2048]{1,0:T(8,128)(2,1)} %get-tuple-element.119), channel_id=1, source_target_pairs={{0,4},{2,6},{4,0},{6,2},{1,5},{3,7},{5,1},{7,3},{8,12},{10,14},{12... | collective-permute-start | bytes 2359304 | tf_op jit(solution)/shard_map/ppermute | solution.py:22
  576.4 26.0 %collective-permute-start.37 = (bf16[192,2048]{1,0:T(8,128)(2,1)S(1)}, bf16[192,2048]{1,0:T(8,128)(2,1)S(1)}, u32[]{:S(2)}, u32[]{:S(2)}) collective-permute-start(bf16[192,2048]{1,0:T(8,128)(2,1)S(1)} %copy-done.21), channel_id=1, source_target_pairs={{0,2},{2,0},{4,6},{6,4},{1,3},{3,1},{5,7},{7,5},{8,10},{10,8},{12,... | collective-permute-start | bytes 2359304 | tf_op jit(solution)/shard_map/ppermute | solution.py:22
  577.5 29.1 %collective-permute-start.63 = (bf16[256,1024]{1,0:T(8,128)(2,1)S(1)}, bf16[256,1024]{1,0:T(8,128)(2,1)S(1)}, u32[]{:S(2)}, u32[]{:S(2)}) collective-permute-start(bf16[256,1024]{1,0:T(8,128)(2,1)S(1)} %copy-done.23), channel_id=1, source_target_pairs={{0,16},{8,24},{16,0},{24,8},{1,17},{9,25},{17,1},{25,9},{2,18},{10... | collective-permute-start | bytes 1572872 | tf_op jit(solution)/shard_map/ppermute | solution.py:22
  598.1 25.9 %collective-permute-start.62 = (bf16[256,1024]{1,0:T(8,128)(2,1)S(1)}, bf16[256,1024]{1,0:T(8,128)(2,1)S(1)}, u32[]{:S(2)}, u32[]{:S(2)}) collective-permute-start(bf16[256,1024]{1,0:T(8,128)(2,1)S(1)} %copy-done.22), channel_id=1, source_target_pairs={{0,8},{8,0},{16,24},{24,16},{1,9},{9,1},{17,25},{25,17},{2,10},{10... | collective-permute-start | bytes 1572872 | tf_op jit(solution)/shard_map/ppermute | solution.py:22
  (92 other events, 1003.3 us)
Sparse Core Ops, SparseCore 0:
  10.2 58.6 all-gather.3
  70.6 77.8 all-gather.5
  150.1 90.9 all-gather.7
  378.6 83.0 reduce-scatter.4
  463.9 109.5 reduce-scatter.2

commit v3 on v2

--- a/solution.py
+++ b/solution.py
@@ -57,7 +57,7 @@
 
 def collect_crossed(value, axis, *others):
     if lax.axis_size(axis) != 4:
-        return after(jnp.concatenate(collect(value, axis), 0), *others)
+        return after(jnp.concatenate(collect(value, axis), 0), *others), ()
     half = value.shape[1] // 2
     low, high = value[:, :half], value[:, half:]
 
@@ -66,9 +66,9 @@
 
     low_1, high_2 = send(low, 1), send(high, 2)
     high_1, low_2 = send(high, 1), send(low, 2)
-    low_3, high_3 = swap(low_1, axis, 2), swap(high_2, axis, 1)
+    low_3, high_3 = send(low_1, 2), send(high_2, 1)
     parts = (low, high, low_1, high_1, low_2, high_2, low_3, high_3)
-    return join(lax.optimization_barrier((*parts, *others))[: len(parts)])
+    return join(lax.optimization_barrier((*parts, *others))[: len(parts)]), (low_1, high_2)
 
 
 def folded_positions(rows, count_ctx, half_block):
@@ -504,7 +504,7 @@
     inverse_two = inv_rms(hidden)
     hat_two = hidden * inverse_two
     normed_two = (hat_two * gain_mlp).astype(BF)
-    arrived = collect_crossed(normed_two, "shard", kv_weights)
+    arrived, _ = collect_crossed(normed_two, "shard", kv_weights)
 
     full_gate_up = full_experts[:, : 2 * hidden_width]
     full_down = full_experts[:, 2 * hidden_width :]
@@ -526,22 +526,16 @@
     grad_hidden = grad_top.astype(F32) + norm_backward_step(
         grad_normed_two, hat_two, inverse_two, gain_mlp
     )
-    expert_out = mm_nt(inner_bf, full_down).astype(BF).astype(F32)
+    grad_hidden_bf = after(grad_hidden.astype(BF), grad_w_experts)
+    grad_att, first_in = collect_crossed(grad_hidden_bf, "shard")
+    expert_out = mm_nt(after(inner_bf, *first_in), full_down).astype(BF).astype(F32)
     weighted = coef * expert_out
     weighted = weighted.astype(BF)
     route_part = jnp.sum(grad_all.astype(F32) * expert_out, -1)
-    grad_hidden_bf = after(grad_hidden.astype(BF), grad_w_experts)
-    grad_att = collect_crossed(grad_hidden_bf, "shard")
-    grad_att, weighted = lax.optimization_barrier((grad_att, weighted))
-    mixture = reduce_blocks(block_rows_of(weighted), False)
+    weighted = [weighted[k * own_rows : (k + 1) * own_rows] for k in range(count_s)]
+    grad_att, *weighted = lax.optimization_barrier((grad_att, *weighted))
+    mixture = reduce_blocks(lambda k, columns: weighted[k], False)
     block_out = (hidden + mixture).astype(BF)
-    route_all = {0: route_part[:own_rows]}
-    for k in order_of(count_s):
-        route_all[k] = swap(route_part[k * own_rows : (k + 1) * own_rows], "shard", k)
-    route_grad = jnp.zeros(ids.shape, F32)
-    for k in range(count_s):
-        route_grad = jnp.where(ids == (me_s ^ k), route_all[k][:, None], route_grad)
-
     attention_gradient = mm(grad_att, full_out).astype(BF)
 
     grad_q, grad_kv, gain_q_parts = pl.pallas_call(
@@ -581,14 +575,15 @@
     grad_kv = grad_kv.reshape(count_c, 2, all_rows, head_dim)
     grad_q = grad_q.reshape(all_rows, q_width)
     grad_w_query = mm_tn(normed_one, grad_q).astype(BF)
-    sum_query = scatter(grad_w_query).astype(F32)
-    query_part = reduce_blocks(
-        lambda k, columns: mm_nt(grad_q[k * own_rows : (k + 1) * own_rows], full_query[columns]),
-        False,
-    )
+    sum_query = scatter(grad_w_query)
+
+    def query_term(k, columns):
+        return mm_nt(grad_q[k * own_rows : (k + 1) * own_rows], full_query[columns])
+
+    query_part = reduce_blocks(query_term, False)
+
     grad_w_out = mm_tn(after(grad_att, grad_kv), attn.reshape(all_rows, q_width)).astype(BF)
     half_sum_out = sum_cores(grad_w_out)
-
     kv_parts = [grad_kv[0]]
     for k in range(1, count_c):
         kv_parts.append(swap(grad_kv[k], "ctx", k))
@@ -607,7 +602,6 @@
     }
     kv_rows[0] = grad_kv_bf[:own_rows]
     half_sum_kv = sum_cores(mm_tn(normed_one, grad_kv_bf).astype(BF))
-    sum_kv = sum_ctx(half_sum_kv, sum_query)
     kv_all_rows = jnp.concatenate([kv_rows[k] for k in range(count_s)], 1)
     expert_parts = jnp.split(sum_experts[None], 3, 2)
     kv_all_rows, _, *expert_parts = lax.optimization_barrier(
@@ -615,6 +609,14 @@
     )
     grad_normed_one = query_part + mm_nt(kv_all_rows, kv_weights)
     gain_attn_part = jnp.sum(grad_normed_one * hat_own, 0)
+    route_part = after(route_part, gain_attn_part)
+    route_all = {0: route_part[:own_rows]}
+    for k in order_of(count_s):
+        route_all[k] = swap(route_part[k * own_rows : (k + 1) * own_rows], "shard", k)
+    route_grad = jnp.zeros(ids.shape, F32)
+    for k in range(count_s):
+        route_grad = jnp.where(ids == (me_s ^ k), route_all[k][:, None], route_grad)
+
     grad_tokens = grad_hidden + norm_backward_step(
         grad_normed_one, hat_own, inverse_own, gain_attn
     )
@@ -622,12 +624,14 @@
         [gain_attn_part, gain_mlp_part, jnp.sum(gain_q_parts, (0, 1)), gain_k_part[0]]
     ).reshape(-1, head_dim)
     for axis in ("dp", "shard", "ctx"):
-        step = 1
-        while step < lax.axis_size(axis):
-            gains = gains + swap(gains, axis, step)
-            step *= 2
+        terms = collect(gains, axis)
+        while len(terms) > 1:
+            terms = [one + other for one, other in zip(terms[::2], terms[1::2])]
+        gains = terms[0]
         if axis == "shard":
             sum_out = sum_ctx(half_sum_out, gains)
+            sum_kv = sum_ctx(half_sum_kv, gains)
+            sum_query = after(sum_query, gains).astype(F32)
     gains = gains.reshape(-1)
 
     def own_shape(value):

time: 646 us -> 633 us (0.980)
  waiting for transfers between devices: 305 us -> 275 us
  local copies, waits for them, and re-layouts: 27.4 us -> 44.5 us
    reduce_scatter x2, waiting for transfers between devices: 81.3 us -> 0.01 us  [scatter(): return lax.psum_scatter(value, both, scatter_dimension=0, tiled=True)]
    ppermute x64 -> x66, waiting for transfers between devices: 211 us -> 262 us  [swap(): return lax.ppermute(value, axis, pairs(lax.axis_size(axis), k))]
    ppermute x64 -> x66, starting transfers between devices: 95.1 us -> 96.6 us  [swap(): return lax.ppermute(value, axis, pairs(lax.axis_size(axis), k))]
  transfers between devices with their start and end apart: 69 -> 71, of which waited for: 34 -> 30; matrix products, arithmetic and copies ran while one was open for 17% -> 22% of each run, Pallas kernels for 6% -> 8%
where the time goes in v3:
time: 633 us; the launch traced here: 624 us
  waiting for transfers between devices  275 us (43%)
  starting transfers between devices  96.8 us (15%)
  matrix products  83.2 us (13%)
  Pallas kernels  64 us (10%)
  other arithmetic  45.3 us (7%)
  local copies, waits for them, and re-layouts  44.5 us (7%)
  between operations  15 us (2%)
    ppermute x66, waiting for transfers between devices, swap(): return lax.ppermute(value, axis, pairs(lax.axis_size(axis), k))  262 us
    ppermute x66, starting transfers between devices, swap(): return lax.ppermute(value, axis, pairs(lax.axis_size(axis), k))  96.6 us
    dot_general x15, matrix products, mm_nt(): lax.dot_general(a, b, (((1,), (1,)), ((), ())), preferred_element_type=F32)  39.4 us
    dot_general x5, matrix products, mm(): lax.dot_general(a, b, (((1,), (0,)), ((), ())), preferred_element_type=F32)  26.8 us
    pallas_call x1, Pallas kernels, per_device(): pl.pallas_call(attn_grad_kernel, grid_spec=pltpu.PrefetchScalarGridSpec(n...  19.6 us
    pallas_call x1, Pallas kernels, per_device(): pl.pallas_call(attn_kernel, grid_spec=pltpu.PrefetchScalarGridSpec(num_sc...  17.4 us
    dot_general x3, matrix products, mm_tn(): lax.dot_general(a, b, (((0,), (0,)), ((), ())), preferred_element_type=F32)  17.1 us
    pallas_call x1, Pallas kernels, expert_grads(): pl.pallas_call(expert_grad_kernel, grid=(width // tile,), in_specs=[pl.Bl...  13.9 us
  transfers between devices with their start and end apart: 71, of which 30 were waited for; matrix products, arithmetic and copies ran while one was open for 22% of the time, Pallas kernels for 8%

profile of v3, /device:TPU:0, one launch (start us, length us, event | category | flops | bytes accessed | tf_op | source)
XLA Modules:
  0.0 623.7 jit_solution(3694993501186050041)
XLA Ops:
  24.4 6.3 %fusion.2 = bf16[768,2048]{1,0:T(8,128)(2,1)} fusion(f32[2048]{0:T(1024)S(1)} %copy-done.42, f32[768]{0:T(1024)S(1)} %add_rsqrt_fusion, bf16[192,2048]{1,0:T(8,128)(2,1)S(1)} %bitcast.143, bf16[192,2048]{1,0:T(8,128)(2,1)S(1)} %bitcast.145, bf16[192,2048]{1,0:T(8,128)(2,1)S(1)} %bitcast.141, bf16[192,2048]{1,0:T(8,128)(2,1)S(1)} %bitcast.132), kind=kLoop, calls=%fused_computation.7 | loop fusion | flops 17301504 | bytes 6302720 | tf_op jit(solution)/shard_map/convert_element_type | solution.py:386
  31.6 18.2 %collective-permute-done.2 = f32[192]{0:T(256)S(1)} collective-permute-done((f32[192]{0:T(256)S(1)}, f32[192]{0:T(256)S(1)}, u32[]{:S(2)}, u32[]{:S(2)}) %collective-permute-start.2) | collective-permute-done | bytes 800 | tf_op jit(solution)/shard_map/ppermute | solution.py:22
  57.2 11.8 %all-gather.4.cloned.1.call-done = bf16[2048,1280]{1,0:T(8,128)(2,1)} async-done(((bf16[256,1280]{1,0:T(8,128)(2,1)}), bf16[2048,1280]{1,0:T(8,128)(2,1)}) %all-gather.4.cloned.1.call-update) | async-done | bytes 5242896 | tf_op jit(solution)/shard_map/all_gather | solution.py:349
  84.1 5.1 fusion.88
  93.8 5.5 collective-permute-done.8
  99.3 46.6 %collective-permute-done.7 = bf16[2,768,128]{2,1,0:T(8,128)(2,1)S(1)} collective-permute-done((bf16[2,768,128]{2,1,0:T(8,128)(2,1)}, bf16[2,768,128]{2,1,0:T(8,128)(2,1)S(1)}, u32[]{:S(2)}, u32[]{:S(2)}) %collective-permute-start.7) | collective-permute-done | bytes 393248 | tf_op jit(solution)/shard_map/ppermute | solution.py:22
  147.2 17.4 %attn_fwd.1 = (bf16[4,3,64,1024]{3,2,1,0:T(8,128)(2,1)}, f32[3,8,256]{2,1,0:T(8,128)}, bf16[3,256,1024]{2,1,0:T(8,128)(2,1)}) custom-call(s32[2]{0:T(128)} %pad_add_fusion.ids_ref, f32[4,3,64,1024]{3,2,1,0:T(8,128)} %bitcast.193, bf16[4,2,4,3,64,128]{5,4,3,2,1,0:T(8,128)(2,1)} %pad_maximum_fusion.4.kv_ref, f32[1,128]{1,0:T(1,128)} %bitcast.191, ...), custom_call_target="tpu_custom_call" | custom-call | flops 3221225472 | bytes 12582912 | tf_op jit(solution)/shard_map/attn_fwd/pallas_call | solution.py:448
  190.8 9.4 %collective-permute-done.14 = bf16[192,1024]{1,0:T(8,128)(2,1)S(1)} collective-permute-done((bf16[192,1024]{1,0:T(8,128)(2,1)S(1)}, bf16[192,1024]{1,0:T(8,128)(2,1)S(1)}, u32[]{:S(2)}, u32[]{:S(2)}) %collective-permute-start.14) | collective-permute-done | bytes 393248 | tf_op jit(solution)/shard_map/ppermute | solution.py:22
  207.5 14.3 %collective-permute-done.22 = bf16[2048,256]{1,0:T(8,128)(2,1)} collective-permute-done((bf16[2048,256]{1,0:T(8,128)(2,1)}, bf16[2048,256]{1,0:T(8,128)(2,1)}, u32[]{:S(2)}, u32[]{:S(2)}) %collective-permute-start.22) | collective-permute-done | bytes 1048608 | tf_op jit(solution)/shard_map/ppermute | solution.py:22
  223.4 11.4 %collective-permute-done.15.refs_2_ = bf16[192,1024]{1,0:T(8,128)(2,1)S(1)} collective-permute-done((bf16[192,1024]{1,0:T(8,128)(2,1)S(1)}, bf16[192,1024]{1,0:T(8,128)(2,1)S(1)}, u32[]{:S(2)}, u32[]{:S(2)}) %collective-permute-start.15) | collective-permute-done | bytes 393248 | tf_op jit(solution)/shard_map/ppermute | solution.py:22
  237.9 5.4 collective-permute-done.16.refs_3_
  251.7 8.7 %fusion.8 = f32[768,1536]{1,0:T(8,128)S(1)} fusion(bf16[768,2048]{1,0:T(8,128)(2,1)} %join.2.rows_ref, bf16[2048,2304]{1,0:T(8,128)(2,1)} %all-gather.8.cloned.1.call-done), kind=kOutput, calls=%fused_computation.13 | convolution fusion | flops 4831838208 | bytes 14155776 | tf_op jit(solution)/shard_map/dot_general | solution.py:100
  266.5 6.5 %fusion.6 = bf16[768,2048]{1,0:T(8,128)(2,1)} fusion(bf16[2048,2304]{1,0:T(8,128)(2,1)S(1)} %copy-done.60, bf16[768,768]{1,0:T(8,128)(2,1)S(1)} %get-tuple-element.126, bf16[768,768]{1,0:T(8,128)(2,1)S(1)} %get-tuple-element.125), kind=kOutput, calls=%fused_computation.11 | convolution fusion | flops 4836556800 | bytes 11796480 | tf_op jit(solution)/shard_map/dot_general | solution.py:104
  273.0 13.9 %expert_grads.1 = bf16[2048,2304]{1,0:T(8,128)(2,1)} custom-call(bf16[768,2048]{1,0:T(8,128)(2,1)} %join.2.rows_ref, bf16[768,2048]{1,0:T(8,128)(2,1)} %fusion.3.grad_in_ref, bf16[768,1536]{1,0:T(8,128)(2,1)} %pad_maximum_fusion.3.grads_ref, bf16[768,768]{1,0:T(8,128)(2,1)} %get-tuple-element.84.inner_ref), custom_call_target="tpu_custom_call" | custom-call | flops 7247757312 | bytes 25165824 | tf_op jit(solution)/shard_map/expert_grads/pallas_call | solution.py:293
  292.1 8.1 %collective-permute-done.25 = bf16[192,1024]{1,0:T(8,128)(2,1)S(1)} collective-permute-done((bf16[192,1024]{1,0:T(8,128)(2,1)S(1)}, bf16[192,1024]{1,0:T(8,128)(2,1)S(1)}, u32[]{:S(2)}, u32[]{:S(2)}) %collective-permute-start.25) | collective-permute-done | bytes 393248 | tf_op jit(solution)/shard_map/ppermute | solution.py:22
  304.4 6.7 %collective-permute-done.26 = bf16[192,1024]{1,0:T(8,128)(2,1)S(1)} collective-permute-done((bf16[192,1024]{1,0:T(8,128)(2,1)S(1)}, bf16[192,1024]{1,0:T(8,128)(2,1)S(1)}, u32[]{:S(2)}, u32[]{:S(2)}) %collective-permute-start.26) | collective-permute-done | bytes 393248 | tf_op jit(solution)/shard_map/ppermute | solution.py:22
  329.6 7.7 %collective-permute-done.30.refs_2_ = bf16[192,1024]{1,0:T(8,128)(2,1)} collective-permute-done((bf16[192,1024]{1,0:T(8,128)(2,1)}, bf16[192,1024]{1,0:T(8,128)(2,1)}, u32[]{:S(2)}, u32[]{:S(2)}) %collective-permute-start.30) | collective-permute-done | bytes 393248 | tf_op jit(solution)/shard_map/ppermute | solution.py:22
  339.4 6.2 %fusion.5 = (f32[768]{0:T(1024)}, bf16[768,2048]{1,0:T(8,128)(2,1)S(1)}) fusion(bf16[192,2048]{1,0:T(8,128)(2,1)} %copy-done.22, bf16[192,2048]{1,0:T(8,128)(2,1)} %copy-done.23, bf16[192,2048]{1,0:T(8,128)(2,1)} %collective-permute-done.3, bf16[192,2048]{1,0:T(8,128)(2,1)} %bitcast.152, f32[768]{0:T(1024)} %copy-done.46, ...), kind=kOutput, calls=%fused_computation.10 | convolution fusion | flops 2437938432 | bytes 10624000 | tf_op jit(solution)/shard_map/dot_general | solution.py:104
  353.1 6.0 convolution_convert_fusion.1
  363.2 4.6 convolution_convert_fusion.7
  367.8 19.6 %attn_bwd.1 = (bf16[4,3,64,1024]{3,2,1,0:T(8,128)(2,1)}, bf16[4,2,4,3,64,128]{5,4,3,2,1,0:T(8,128)(2,1)}, f32[3,1,128]{2,1,0:T(1,128)}) custom-call(s32[2]{0:T(128)} %pad_add_fusion.ids_ref, bf16[3,256,1024]{2,1,0:T(8,128)(2,1)} %get-tuple-element.89.qb_ref, f32[4,3,64,1024]{3,2,1,0:T(8,128)} %bitcast.194, ...), custom_call_target="tpu_custom_call" | custom-call | flops 8053063680 | bytes 25165824 | tf_op jit(solution)/shard_map/attn_bwd/pallas_call | solution.py:541
  387.4 7.9 %convolution_convert_fusion = bf16[2048,1024]{1,0:T(8,128)(2,1)} fusion(bf16[768,2048]{1,0:T(8,128)(2,1)} %fusion.2, bf16[768,1024]{1,0:T(8,128)(2,1)} %bitcast.159), kind=kOutput, calls=%fused_computation.18 | convolution fusion | flops 3223322624 | bytes 8912896 | tf_op jit(solution)/shard_map/dot_general | solution.py:108
  398.3 4.8 convolution_convert_fusion.4
  421.6 15.2 %collective-permute-done.42.refs_1_ = bf16[2,768,128]{2,1,0:T(8,128)(2,1)S(1)} collective-permute-done((bf16[2,768,128]{2,1,0:T(8,128)(2,1)S(1)}, bf16[2,768,128]{2,1,0:T(8,128)(2,1)S(1)}, u32[]{:S(2)}, u32[]{:S(2)}) %collective-permute-start.42) | collective-permute-done | bytes 393248 | tf_op jit(solution)/shard_map/ppermute | solution.py:22
  436.8 4.5 collective-permute-done.43.refs_2_
  441.2 21.1 %collective-permute-done.44.refs_3_ = bf16[2,768,128]{2,1,0:T(8,128)(2,1)S(1)} collective-permute-done((bf16[2,768,128]{2,1,0:T(8,128)(2,1)S(1)}, bf16[2,768,128]{2,1,0:T(8,128)(2,1)S(1)}, u32[]{:S(2)}, u32[]{:S(2)}) %collective-permute-start.44) | collective-permute-done | bytes 393248 | tf_op jit(solution)/shard_map/ppermute | solution.py:22
  495.4 7.3 %collective-permute-done.40 = bf16[192,2048]{1,0:T(8,128)(2,1)} collective-permute-done((bf16[192,2048]{1,0:T(8,128)(2,1)}, bf16[192,2048]{1,0:T(8,128)(2,1)}, u32[]{:S(2)}, u32[]{:S(2)}) %collective-permute-start.40) | collective-permute-done | bytes 786464 | tf_op jit(solution)/shard_map/ppermute | solution.py:22
  502.7 18.3 %collective-permute-done.39 = bf16[192,2048]{1,0:T(8,128)(2,1)} collective-permute-done((bf16[192,2048]{1,0:T(8,128)(2,1)}, bf16[192,2048]{1,0:T(8,128)(2,1)}, u32[]{:S(2)}, u32[]{:S(2)}) %collective-permute-start.39) | collective-permute-done | bytes 786464 | tf_op jit(solution)/shard_map/ppermute | solution.py:22
  530.0 6.5 %collective-permute-done.37 = bf16[192,2048]{1,0:T(8,128)(2,1)} collective-permute-done((bf16[192,2048]{1,0:T(8,128)(2,1)}, bf16[192,2048]{1,0:T(8,128)(2,1)}, u32[]{:S(2)}, u32[]{:S(2)}) %collective-permute-start.37) | collective-permute-done | bytes 786464 | tf_op jit(solution)/shard_map/ppermute | solution.py:22
  536.5 16.4 %collective-permute-done.36 = bf16[192,2048]{1,0:T(8,128)(2,1)S(1)} collective-permute-done((bf16[192,2048]{1,0:T(8,128)(2,1)S(1)}, bf16[192,2048]{1,0:T(8,128)(2,1)S(1)}, u32[]{:S(2)}, u32[]{:S(2)}) %collective-permute-start.36) | collective-permute-done | bytes 786464 | tf_op jit(solution)/shard_map/ppermute | solution.py:22
  552.9 10.9 %collective-permute-start.64 = (bf16[256,1024]{1,0:T(8,128)(2,1)}, bf16[256,1024]{1,0:T(8,128)(2,1)}, u32[]{:S(2)}, u32[]{:S(2)}) collective-permute-start(bf16[256,1024]{1,0:T(8,128)(2,1)} %get-tuple-element.148), channel_id=1, source_target_pairs={{0,8},{8,0},{16,24},{24,16},{1,9},{9,1},{17,25},{25,17},{2,10},{10... | collective-permute-start | bytes 1572872 | tf_op jit(solution)/shard_map/ppermute | solution.py:22
  574.0 16.5 %collective-permute-done.60 = bf16[256,256]{1,0:T(8,128)(2,1)S(1)} collective-permute-done((bf16[256,256]{1,0:T(8,128)(2,1)}, bf16[256,256]{1,0:T(8,128)(2,1)S(1)}, u32[]{:S(2)}, u32[]{:S(2)}) %collective-permute-start.60) | collective-permute-done | bytes 131104 | tf_op jit(solution)/shard_map/ppermute | solution.py:22
  (350 shorter events, 240.0 us)
Async XLA Ops:
  7.2 61.8 %all-gather.4.cloned.1.call-start = ((), (), s32[]{:S(2)}) async-start(), calls=%async_computation.2 | async-start | bytes 5898240 | tf_op jit(solution)/shard_map/all_gather | solution.py:349
  9.4 156.8 %all-gather.6.cloned.1.call-start = ((), (), s32[]{:S(2)}) async-start(), calls=%async_computation.3 | async-start | bytes 4718592 | tf_op jit(solution)/shard_map/all_gather | solution.py:349
  10.1 241.6 %all-gather.8.cloned.1.call-start = ((), (), s32[]{:S(2)}) async-start(), calls=%async_computation.4 | async-start | bytes 10616832 | tf_op jit(solution)/shard_map/all_gather | solution.py:349
  11.4 479.2 %reduce-scatter.3.cloned.1.call-start = ((), (), s32[]{:S(2)}) async-start(), calls=%async_computation.5 | async-start | bytes 10616832 | tf_op jit(solution)/shard_map/reduce_scatter | solution.py:352
  11.4 42.1 %collective-permute-start.5 = (bf16[192,2048]{1,0:T(8,128)(2,1)S(1)}, bf16[192,2048]{1,0:T(8,128)(2,1)S(1)}, u32[]{:S(2)}, u32[]{:S(2)}) collective-permute-start(bf16[192,2048]{1,0:T(8,128)(2,1)S(1)} %bitcast.153), channel_id=1, source_target_pairs={{0,6},{2,4},{4,2},{6,0},{1,7},{3,5},{5,3},{7,1},{8,14},{10,12},{12... | collective-permute-start | bytes 2359304 | tf_op jit(solution)/shard_map/ppermute | solution.py:22
  15.4 38.1 %collective-permute-start.4 = (bf16[192,2048]{1,0:T(8,128)(2,1)S(1)}, bf16[192,2048]{1,0:T(8,128)(2,1)S(1)}, u32[]{:S(2)}, u32[]{:S(2)}) collective-permute-start(bf16[192,2048]{1,0:T(8,128)(2,1)S(1)} %bitcast.154), channel_id=1, source_target_pairs={{0,4},{2,6},{4,0},{6,2},{1,5},{3,7},{5,1},{7,3},{8,12},{10,14},{12... | collective-permute-start | bytes 2359304 | tf_op jit(solution)/shard_map/ppermute | solution.py:22
  15.9 37.6 %collective-permute-start.3 = (bf16[192,2048]{1,0:T(8,128)(2,1)S(1)}, bf16[192,2048]{1,0:T(8,128)(2,1)}, u32[]{:S(2)}, u32[]{:S(2)}) collective-permute-start(bf16[192,2048]{1,0:T(8,128)(2,1)S(1)} %bitcast.155), channel_id=1, source_target_pairs={{0,2},{2,0},{4,6},{6,4},{1,3},{3,1},{5,7},{7,5},{8,10},{10,8},{12,... | collective-permute-start | bytes 2359304 | tf_op jit(solution)/shard_map/ppermute | solution.py:22
  16.2 33.7 %collective-permute-start.2 = (f32[192]{0:T(256)S(1)}, f32[192]{0:T(256)S(1)}, u32[]{:S(2)}, u32[]{:S(2)}) collective-permute-start(f32[192]{0:T(256)S(1)} %reduce_sum.133), channel_id=1, source_target_pairs={{0,6},{2,4},{4,2},{6,0},{1,7},{3,5},{5,3},{7,1},{8,14},{10,12},{12... | collective-permute-start | bytes 2312 | tf_op jit(solution)/shard_map/ppermute | solution.py:22
  19.1 33.2 %collective-permute-start.1 = (f32[192]{0:T(256)S(1)}, f32[192]{0:T(256)S(1)}, u32[]{:S(2)}, u32[]{:S(2)}) collective-permute-start(f32[192]{0:T(256)S(1)} %reduce_sum.131), channel_id=1, source_target_pairs={{0,4},{2,6},{4,0},{6,2},{1,5},{3,7},{5,1},{7,3},{8,12},{10,14},{12... | collective-permute-start | bytes 2312 | tf_op jit(solution)/shard_map/ppermute | solution.py:22
  77.8 68.0 %collective-permute-start.7 = (bf16[2,768,128]{2,1,0:T(8,128)(2,1)}, bf16[2,768,128]{2,1,0:T(8,128)(2,1)S(1)}, u32[]{:S(2)}, u32[]{:S(2)}) collective-permute-start(bf16[2,768,128]{2,1,0:T(8,128)(2,1)} %key_prep.1), channel_id=1, source_target_pairs={{0,16},{8,24},{16,0},{24,8},{1,17},{9,25},{17,1},{25,9},{2,18},{10... | collective-permute-start | bytes 1179656 | tf_op jit(solution)/shard_map/ppermute | solution.py:22
  78.3 67.6 %collective-permute-start.6 = (bf16[2,768,128]{2,1,0:T(8,128)(2,1)}, bf16[2,768,128]{2,1,0:T(8,128)(2,1)S(1)}, u32[]{:S(2)}, u32[]{:S(2)}) collective-permute-start(bf16[2,768,128]{2,1,0:T(8,128)(2,1)} %key_prep.1), channel_id=1, source_target_pairs={{0,8},{8,0},{16,24},{24,16},{1,9},{9,1},{17,25},{25,17},{2,10},{10... | collective-permute-start | bytes 1179656 | tf_op jit(solution)/shard_map/ppermute | solution.py:22
  91.5 114.5 %collective-permute-start.23 = (bf16[2048,256]{1,0:T(8,128)(2,1)}, bf16[2048,256]{1,0:T(8,128)(2,1)}, u32[]{:S(2)}, u32[]{:S(2)}) collective-permute-start(bf16[2048,256]{1,0:T(8,128)(2,1)} %slice.254), channel_id=1, source_target_pairs={{0,6},{2,4},{4,2},{6,0},{1,7},{3,5},{5,3},{7,1},{8,14},{10,12},{12... | collective-permute-start | bytes 3145736 | tf_op jit(solution)/shard_map/ppermute | solution.py:22
  189.7 32.1 %collective-permute-start.22 = (bf16[2048,256]{1,0:T(8,128)(2,1)}, bf16[2048,256]{1,0:T(8,128)(2,1)}, u32[]{:S(2)}, u32[]{:S(2)}) collective-permute-start(bf16[2048,256]{1,0:T(8,128)(2,1)} %slice.254), channel_id=1, source_target_pairs={{0,4},{2,6},{4,0},{6,2},{1,5},{3,7},{5,1},{7,3},{8,12},{10,14},{12... | collective-permute-start | bytes 3145736 | tf_op jit(solution)/shard_map/ppermute | solution.py:22
  200.2 37.7 %collective-permute-start.21 = (bf16[2048,256]{1,0:T(8,128)(2,1)}, bf16[2048,256]{1,0:T(8,128)(2,1)}, u32[]{:S(2)}, u32[]{:S(2)}) collective-permute-start(bf16[2048,256]{1,0:T(8,128)(2,1)} %slice.254), channel_id=1, source_target_pairs={{0,2},{2,0},{4,6},{6,4},{1,3},{3,1},{5,7},{7,5},{8,10},{10,8},{12,... | collective-permute-start | bytes 3145736 | tf_op jit(solution)/shard_map/ppermute | solution.py:22
  204.5 31.9 %collective-permute-start.18 = (bf16[192,1024]{1,0:T(8,128)(2,1)S(1)}, bf16[192,1024]{1,0:T(8,128)(2,1)S(1)}, u32[]{:S(2)}, u32[]{:S(2)}) collective-permute-start(bf16[192,1024]{1,0:T(8,128)(2,1)S(1)} %get-tuple-element.67.refs_1_), channel_id=1, source_target_pairs={{0,4},{2,6},{4,0},{6,2},{1,5},{3,7},{5,1},{7,3},{8,12},{10,14},{12... | collective-permute-start | bytes 1179656 | tf_op jit(solution)/shard_map/ppermute | solution.py:22
  206.0 37.2 %collective-permute-start.16 = (bf16[192,1024]{1,0:T(8,128)(2,1)S(1)}, bf16[192,1024]{1,0:T(8,128)(2,1)S(1)}, u32[]{:S(2)}, u32[]{:S(2)}) collective-permute-start(bf16[192,1024]{1,0:T(8,128)(2,1)S(1)} %get-tuple-element.67.refs_1_), channel_id=1, source_target_pairs={{0,2},{2,0},{4,6},{6,4},{1,3},{3,1},{5,7},{7,5},{8,10},{10,8},{12,... | collective-permute-start | bytes 1179656 | tf_op jit(solution)/shard_map/ppermute | solution.py:22
  286.9 326.6 %reduce-scatter.5.cloned.1.call-start = ((), (), s32[]{:S(2)}) async-start(), calls=%async_computation.6 | async-start | bytes 4718592 | tf_op jit(solution)/shard_map/reduce_scatter | solution.py:352
  360.6 57.0 %collective-permute-start.45 = (bf16[4,256,1024]{2,1,0:T(8,128)(2,1)}, bf16[4,256,1024]{2,1,0:T(8,128)(2,1)}, u32[]{:S(2)}, u32[]{:S(2)}) collective-permute-start(bf16[4,256,1024]{2,1,0:T(8,128)(2,1)} %dynamic-slice_bitcast_fusion), channel_id=1, source_target_pairs={{0,1},{1,0},{2,3},{3,2},{4,5},{5,4},{6,7},{7,6},{8,9},{9,8},{10,11... | collective-permute-start | bytes 6291464 | tf_op jit(solution)/shard_map/ppermute | solution.py:22
  403.1 90.4 %collective-permute-start.41 = (bf16[192,2048]{1,0:T(8,128)(2,1)}, bf16[192,2048]{1,0:T(8,128)(2,1)}, u32[]{:S(2)}, u32[]{:S(2)}) collective-permute-start(bf16[192,2048]{1,0:T(8,128)(2,1)} %convolution_convert_fusion.4), channel_id=1, source_target_pairs={{0,4},{2,6},{4,0},{6,2},{1,5},{3,7},{5,1},{7,3},{8,12},{10,14},{12... | collective-permute-start | bytes 2359304 | tf_op jit(solution)/shard_map/ppermute | solution.py:22
  404.7 32.0 %collective-permute-start.42 = (bf16[2,768,128]{2,1,0:T(8,128)(2,1)S(1)}, bf16[2,768,128]{2,1,0:T(8,128)(2,1)S(1)}, u32[]{:S(2)}, u32[]{:S(2)}) collective-permute-start(bf16[2,768,128]{2,1,0:T(8,128)(2,1)S(1)} %bitcast.180), channel_id=1, source_target_pairs={{0,8},{8,0},{16,24},{24,16},{1,9},{9,1},{17,25},{25,17},{2,10},{10... | collective-permute-start | bytes 1179656 | tf_op jit(solution)/shard_map/ppermute | solution.py:22
  408.9 32.3 %collective-permute-start.43 = (bf16[2,768,128]{2,1,0:T(8,128)(2,1)S(1)}, bf16[2,768,128]{2,1,0:T(8,128)(2,1)S(1)}, u32[]{:S(2)}, u32[]{:S(2)}) collective-permute-start(bf16[2,768,128]{2,1,0:T(8,128)(2,1)S(1)} %bitcast.179), channel_id=1, source_target_pairs={{0,16},{8,24},{16,0},{24,8},{1,17},{9,25},{17,1},{25,9},{2,18},{10... | collective-permute-start | bytes 1179656 | tf_op jit(solution)/shard_map/ppermute | solution.py:22
  412.5 49.8 %collective-permute-start.44 = (bf16[2,768,128]{2,1,0:T(8,128)(2,1)S(1)}, bf16[2,768,128]{2,1,0:T(8,128)(2,1)S(1)}, u32[]{:S(2)}, u32[]{:S(2)}) collective-permute-start(bf16[2,768,128]{2,1,0:T(8,128)(2,1)S(1)} %bitcast.176), channel_id=1, source_target_pairs={{0,24},{8,16},{16,8},{24,0},{1,25},{9,17},{17,9},{25,1},{2,26},{10... | collective-permute-start | bytes 1179656 | tf_op jit(solution)/shard_map/ppermute | solution.py:22
  484.0 37.0 %collective-permute-start.39 = (bf16[192,2048]{1,0:T(8,128)(2,1)}, bf16[192,2048]{1,0:T(8,128)(2,1)}, u32[]{:S(2)}, u32[]{:S(2)}) collective-permute-start(bf16[192,2048]{1,0:T(8,128)(2,1)} %convolution_convert_fusion.6), channel_id=1, source_target_pairs={{0,6},{2,4},{4,2},{6,0},{1,7},{3,5},{5,3},{7,1},{8,14},{10,12},{12... | collective-permute-start | bytes 2359304 | tf_op jit(solution)/shard_map/ppermute | solution.py:22
  485.8 41.7 %collective-permute-start.38 = (bf16[192,2048]{1,0:T(8,128)(2,1)}, bf16[192,2048]{1,0:T(8,128)(2,1)}, u32[]{:S(2)}, u32[]{:S(2)}) collective-permute-start(bf16[192,2048]{1,0:T(8,128)(2,1)} %get-tuple-element.88), channel_id=1, source_target_pairs={{0,4},{2,6},{4,0},{6,2},{1,5},{3,7},{5,1},{7,3},{8,12},{10,14},{12... | collective-permute-start | bytes 2359304 | tf_op jit(solution)/shard_map/ppermute | solution.py:22
  487.2 49.3 %collective-permute-start.37 = (bf16[192,2048]{1,0:T(8,128)(2,1)}, bf16[192,2048]{1,0:T(8,128)(2,1)}, u32[]{:S(2)}, u32[]{:S(2)}) collective-permute-start(bf16[192,2048]{1,0:T(8,128)(2,1)} %get-tuple-element.87), channel_id=1, source_target_pairs={{0,2},{2,0},{4,6},{6,4},{1,3},{3,1},{5,7},{7,5},{8,10},{10,8},{12,... | collective-permute-start | bytes 2359304 | tf_op jit(solution)/shard_map/ppermute | solution.py:22
  493.5 59.3 %collective-permute-start.36 = (bf16[192,2048]{1,0:T(8,128)(2,1)S(1)}, bf16[192,2048]{1,0:T(8,128)(2,1)S(1)}, u32[]{:S(2)}, u32[]{:S(2)}) collective-permute-start(bf16[192,2048]{1,0:T(8,128)(2,1)S(1)} %copy-done.21), channel_id=1, source_target_pairs={{0,6},{2,4},{4,2},{6,0},{1,7},{3,5},{5,3},{7,1},{8,14},{10,12},{12... | collective-permute-start | bytes 2359304 | tf_op jit(solution)/shard_map/ppermute | solution.py:22
  525.9 37.9 %collective-permute-start.52 = (f32[192]{0:T(256)S(1)}, f32[192]{0:T(256)S(1)}, u32[]{:S(2)}, u32[]{:S(2)}) collective-permute-start(f32[192]{0:T(256)S(1)} %get-tuple-element.183), channel_id=1, source_target_pairs={{0,2},{2,0},{4,6},{6,4},{1,3},{3,1},{5,7},{7,5},{8,10},{10,8},{12,... | collective-permute-start | bytes 2312 | tf_op jit(solution)/shard_map/ppermute | solution.py:22
  527.4 37.2 %collective-permute-start.51 = (f32[192]{0:T(256)S(1)}, f32[192]{0:T(256)S(1)}, u32[]{:S(2)}, u32[]{:S(2)}) collective-permute-start(f32[192]{0:T(256)S(1)} %get-tuple-element.184), channel_id=1, source_target_pairs={{0,4},{2,6},{4,0},{6,2},{1,5},{3,7},{5,1},{7,3},{8,12},{10,14},{12... | collective-permute-start | bytes 2312 | tf_op jit(solution)/shard_map/ppermute | solution.py:22
  527.9 38.3 %collective-permute-start.50 = (f32[192]{0:T(256)S(1)}, f32[192]{0:T(256)S(1)}, u32[]{:S(2)}, u32[]{:S(2)}) collective-permute-start(f32[192]{0:T(256)S(1)} %get-tuple-element.181), channel_id=1, source_target_pairs={{0,6},{2,4},{4,2},{6,0},{1,7},{3,5},{5,3},{7,1},{8,14},{10,12},{12... | collective-permute-start | bytes 2312 | tf_op jit(solution)/shard_map/ppermute | solution.py:22
  536.5 72.4 %collective-permute-start.63 = (bf16[256,1024]{1,0:T(8,128)(2,1)}, bf16[256,1024]{1,0:T(8,128)(2,1)}, u32[]{:S(2)}, u32[]{:S(2)}) collective-permute-start(bf16[256,1024]{1,0:T(8,128)(2,1)} %get-tuple-element.149), channel_id=1, source_target_pairs={{0,24},{8,16},{16,8},{24,0},{1,25},{9,17},{17,9},{25,1},{2,26},{10... | collective-permute-start | bytes 1572872 | tf_op jit(solution)/shard_map/ppermute | solution.py:22
  552.9 56.0 %collective-permute-start.64 = (bf16[256,1024]{1,0:T(8,128)(2,1)}, bf16[256,1024]{1,0:T(8,128)(2,1)}, u32[]{:S(2)}, u32[]{:S(2)}) collective-permute-start(bf16[256,1024]{1,0:T(8,128)(2,1)} %get-tuple-element.148), channel_id=1, source_target_pairs={{0,8},{8,0},{16,24},{24,16},{1,9},{9,1},{17,25},{25,17},{2,10},{10... | collective-permute-start | bytes 1572872 | tf_op jit(solution)/shard_map/ppermute | solution.py:22
  563.8 45.1 %collective-permute-start.65 = (bf16[256,1024]{1,0:T(8,128)(2,1)}, bf16[256,1024]{1,0:T(8,128)(2,1)}, u32[]{:S(2)}, u32[]{:S(2)}) collective-permute-start(bf16[256,1024]{1,0:T(8,128)(2,1)} %get-tuple-element.147), channel_id=1, source_target_pairs={{0,16},{8,24},{16,0},{24,8},{1,17},{9,25},{17,1},{25,9},{2,18},{10... | collective-permute-start | bytes 1572872 | tf_op jit(solution)/shard_map/ppermute | solution.py:22
  (102 other events, 1290.7 us)
Sparse Core Ops, SparseCore 0:
  10.2 58.6 all-gather.3
  70.6 77.7 all-gather.5
  150.1 90.9 all-gather.7
  287.0 103.9 reduce-scatter.2
  395.5 84.2 reduce-scatter.4
